TPU v7x, 8 devices: a whole 2x2x1 slice. The times are simulated.
8 devices in a mesh: dp: 2 (over y, z), ep: 4 (over x, core).
Axes of the slice: x: 2, y: 2, z: 1, core: 2. Of those that a mesh axis runs over, the one named last changes fastest.
Arguments:
- x: bfloat16 [2, 4, 512, 4096], P('dp', 'ep'), parts along dimension 0
- expert: int32 [2, 4, 512, 8], P('dp', 'ep'), parts along dimension 0
- slot: int32 [2, 4, 512, 8], P('dp', 'ep'), parts along dimension 0
- gate: float32 [2, 4, 512, 8], P('dp', 'ep'), parts along dimension 0
- w_gate: bfloat16 [64, 4096, 1536], P('ep')
- w_up: bfloat16 [64, 4096, 1536], P('ep')
- w_down: bfloat16 [64, 1536, 4096], P('ep')
Outputs:
- y: bfloat16 [2, 4, 512, 4096], P('dp', 'ep'), parts along dimension 0
There are 2 independent parts. A program takes and returns all parts, laid end to end along the dimension named above; an argument that names none is the same for every part.
All inputs are finite; a program needn't handle non-finite values.
Results may differ from a plain program's by a relative error of at most 0.009.
Values are sent between devices in bfloat16 or wider.
A program may use at most 2 GiB of HBM per device.

v0:
```python
import jax
import jax.numpy as jnp
from jax import lax
from jax.sharding import NamedSharding, PartitionSpec as P


def einsum(form, a, b):
    return jnp.einsum(form, a.astype(jnp.float32), b.astype(jnp.float32))


def solution(mesh):
    def placed(v, *spec):
        return lax.with_sharding_constraint(v, NamedSharding(mesh, P(*spec)))

    def step(x, expert, slot, gate, w_gate, w_up, w_down):
        experts, (tokens, top) = w_gate.shape[0], expert.shape[2:]
        slots = 5 * tokens * top // (4 * experts)
        to_expert = jax.nn.one_hot(expert, experts, dtype=jnp.bfloat16)
        to_slot = jax.nn.one_hot(slot, slots, dtype=jnp.bfloat16)
        weighted = to_expert * gate[..., None].astype(jnp.bfloat16)
        dispatch = einsum("abtke,abtkc->abtec", to_expert, to_slot).astype(jnp.bfloat16)
        combine = einsum("abtke,abtkc->abtec", weighted, to_slot).astype(jnp.bfloat16)
        z = einsum("abtec,abtd->aebcd", dispatch, x).astype(jnp.bfloat16)
        z = placed(z, "dp", None, "ep", None, None)
        z = placed(z, "dp", "ep", None, None, None)
        h = jax.nn.silu(einsum("aebcd,edf->aebcf", z, w_gate))
        h = (h * einsum("aebcd,edf->aebcf", z, w_up)).astype(jnp.bfloat16)
        out = einsum("aebcf,efd->aebcd", h, w_down).astype(jnp.bfloat16)
        out = placed(out, "dp", "ep", None, None, None)
        out = placed(out, "dp", None, "ep", None, None)
        y = einsum("abtec,aebcd->abtd", combine, out)
        return y.astype(jnp.bfloat16)

    return step
```

profile of v0, /device:TPU:0, one launch (start us, length us, event | category | flops | bytes accessed | tf_op | source)
XLA Modules:
  0.0 1429.0 jit_solution(1282585566212014693)
XLA Ops:
  0.0 0.8 copy.11
  0.8 0.0 copy-start
  0.9 0.9 copy.9
  1.7 0.0 copy-start.2
  1.7 8.1 convolution_convert_fusion.1
  9.9 107.2 %convolution_convert_fusion = bf16[64,80,4096]{2,1,0:T(8,128)(2,1)} fusion(bf16[512,64,80]{2,1,0:T(8,128)(2,1)} %convolution_convert_fusion.1, bf16[1,1,512,4096]{3,2,1,0:T(8,128)(2,1)} %param.3), kind=kOutput, calls=%fused_computation.18 | convolution fusion | flops 21495808000 | bytes 51380224 | tf_op jit(solution)/abtec,abtd->aebcd/dot_general | solution.py:8
  117.1 0.0 copy-done
  117.1 0.0 copy-done.2
  117.1 475.1 %all-to-all.4 = bf16[1,4,16,1,80,4096]{5,4,2,3,0,1:T(8,128)(2,1)} all-to-all(bf16[1,4,16,1,80,4096]{5,4,2,3,0,1:T(8,128)(2,1)} %bitcast.84), channel_id=1, replica_groups=mesh['dp'=2,'ep'=4] {'ep'}, dimensions={1} | all-to-all | bytes 83886080 | tf_op jit(solution)/sharding_constraint;jit(solution)/sharding_constraint | solution.py:13
  592.2 93.7 %fusion.2 = f32[16,4,80,1536]{3,2,1,0:T(8,128)} fusion(bf16[16,4096,1536]{2,1,0:T(8,128)(2,1)} %param.5, bf16[1,4,16,1,80,4096]{5,4,2,3,0,1:T(8,128)(2,1)} %all-to-all.4), kind=kOutput, calls=%fused_computation.2 | convolution fusion | flops 64424509440 | bytes 274726912 | tf_op jit(solution)/aebcd,edf->aebcf/dot_general | solution.py:8
  685.9 98.3 %fusion.10 = bf16[1,16,4,80,1536]{4,3,2,1,0:T(8,128)(2,1)} fusion(f32[16,4,80,1536]{3,2,1,0:T(8,128)} %fusion.2, bf16[16,4096,1536]{2,1,0:T(8,128)(2,1)} %param.4, bf16[1,4,16,1,80,4096]{5,4,2,3,0,1:T(8,128)(2,1)} %all-to-all.4), kind=kOutput, calls=%fused_computation.12 | convolution fusion | flops 64471695360 | bytes 290455552 | tf_op jit(solution)/aebcd,edf->aebcf/dot_general | solution.py:8
  784.2 94.8 %convert_bitcast_fusion = bf16[1,16,4,1,80,4096]{5,4,2,1,3,0:T(8,128)(2,1)} fusion(bf16[16,1536,4096]{2,1,0:T(8,128)(2,1)} %param.6, bf16[1,16,4,80,1536]{4,3,2,1,0:T(8,128)(2,1)} %fusion.10), kind=kOutput, calls=%fused_computation.8 | convolution fusion | flops 64445480960 | bytes 258998272 | tf_op jit(solution)/aebcf,efd->aebcd/dot_general | solution.py:8
  879.0 28.0 %copy.15 = bf16[1,16,4,1,80,4096]{5,4,1,3,0,2:T(8,128)(2,1)} copy(bf16[1,16,4,1,80,4096]{5,4,2,1,3,0:T(8,128)(2,1)} %convert_bitcast_fusion) | data formatting | bytes 83886080 | tf_op jit(solution)/sharding_constraint;jit(solution)/sharding_constraint | solution.py:13
  907.0 0.0 copy-start.4
  907.0 0.0 copy-start.1
  907.0 0.0 copy-start.3
  907.0 11.5 all-to-all-start.1
  918.5 0.0 copy-done.4
  918.5 0.2 copy.10
  918.7 0.0 copy-done.1
  918.7 0.0 copy-done.3
  918.7 8.8 convolution_convert_fusion.2
  927.6 443.3 %all-to-all-done.1 = bf16[1,16,4,1,80,4096]{5,4,1,3,0,2:T(8,128)(2,1)} async-done(((bf16[1,16,4,1,80,4096]{5,4,1,3,0,2:T(8,128)(2,1)}), bf16[1,16,4,1,80,4096]{5,4,1,3,0,2:T(8,128)(2,1)}, u32[]{:S(2)}, u32[]{:S(2)}) %all-to-all-start.1) | async-done | bytes 41943072 | tf_op jit(solution)/sharding_constraint;jit(solution)/sharding_constraint | solution.py:13
  1370.9 58.0 %fusion.26 = bf16[1,1,512,4096]{3,2,1,0:T(8,128)(2,1)} fusion(bf16[64,80,4096]{2,1,0:T(8,128)(2,1)} %bitcast.25, bf16[512,64,80]{2,1,0:T(8,128)(2,1)} %convolution_convert_fusion.2), kind=kOutput, calls=%fused_computation.26 | convolution fusion | flops 21476933632 | bytes 51380224 | tf_op jit(solution)/abtec,aebcd->abtd/dot_general | solution.py:8
  (1 shorter events, 0.0 us)
Async XLA Ops:
  0.8 116.3 %copy-start = (s32[512,8]{1,0:T(8,128)}, s32[512,8]{1,0:T(8,128)S(1)}, u32[]{:S(2)}) copy-start(s32[512,8]{1,0:T(8,128)S(1)} %copy.11) | copy-start | bytes 49156
  1.7 115.4 %copy-start.2 = (s32[512,8]{1,0:T(8,128)}, s32[512,8]{1,0:T(8,128)S(1)}, u32[]{:S(2)}) copy-start(s32[512,8]{1,0:T(8,128)S(1)} %copy.9) | copy-start | bytes 49156
  907.0 11.5 copy-start.4
  907.0 11.7 copy-start.1
  907.0 11.7 copy-start.3
  907.0 463.8 %all-to-all-start.1 = ((bf16[1,16,4,1,80,4096]{5,4,1,3,0,2:T(8,128)(2,1)}), bf16[1,16,4,1,80,4096]{5,4,1,3,0,2:T(8,128)(2,1)}, u32[]{:S(2)}, u32[]{:S(2)}) async-start(bf16[1,16,4,1,80,4096]{5,4,1,3,0,2:T(8,128)(2,1)} %copy.15), calls=%async_computation.1 | async-start | bytes 83886080 | tf_op jit(solution)/sharding_constraint;jit(solution)/sharding_constraint | solution.py:13
where the time goes:
time: 1430 us
  blocking collectives  475 us (33%)
  matrix products  469 us (33%)
  waiting for transfers between devices  443 us (31%)
  local copies, waits for them, and re-layouts  29.9 us (2%)
    another operation x1, blocking collectives, placed(): return lax.with_sharding_constraint(v, NamedSharding(mesh, P(*spec)))  475 us
    dot_general x7, matrix products, einsum(): return jnp.einsum(form, a.astype(jnp.float32), b.astype(jnp.float32))  469 us
    another operation x1, waiting for transfers between devices, placed(): return lax.with_sharding_constraint(v, NamedSharding(mesh, P(*spec)))  443 us
  transfers between devices with their start and end apart: 1, of which 1 were waited for; matrix products, arithmetic and copies ran while one was open for 1% of the time, Pallas kernels for 0%

commit v1 on v0

v1 whole, which is shorter than its diff:
```python
import jax
import jax.numpy as jnp
from jax import lax
from jax.experimental import pallas as pl
from jax.experimental.pallas import tpu as pltpu
from jax.sharding import PartitionSpec as P

F32, BF16, I32 = jnp.float32, jnp.bfloat16, jnp.int32
VMEM_LIMIT = 64 * 1024 * 1024 - 64 * 1024 * 2
GROUP = 16
CHUNKS = (1024, 1024, 1024, 512, 512)
ANY = pl.BlockSpec(memory_space=pl.ANY)


def params(*semantics):
    return pltpu.CompilerParams(dimension_semantics=semantics, vmem_limit_bytes=VMEM_LIMIT)


def dispatch(rows_used, place, x, rows):
    top, tokens = place.shape
    d = x.shape[1]
    tile = min(d, 1024)
    block = 256

    def kernel(used_ref, place_ref, x_ref, z_ref, hot_ref):
        @pl.when(pl.program_id(0) == 0)
        def _():
            def build(i, _):
                row = lax.broadcasted_iota(I32, (block, tokens), 0) + i * block
                hit = row == place_ref[0:1, :]
                for k in range(1, top):
                    hit = hit | (row == place_ref[k:k + 1, :])
                hot_ref[pl.ds(pl.multiple_of(i * block, block), block), :] = jnp.where(hit, 1.0, 0.0).astype(BF16)
                return 0

            lax.fori_loop(0, rows // block, build, 0)

        def step(i, _):
            at = pl.ds(pl.multiple_of(i * block, block), block)
            z_ref[at, :] = jnp.dot(hot_ref[at, :], x_ref[...], preferred_element_type=F32).astype(BF16)
            return 0

        lax.fori_loop(0, (used_ref[0] + block - 1) // block, step, 0)

    return pl.pallas_call(
        kernel,
        out_shape=jax.ShapeDtypeStruct((rows, d), BF16),
        grid_spec=pltpu.PrefetchScalarGridSpec(
            num_scalar_prefetch=1,
            grid=(d // tile,),
            in_specs=[
                pl.BlockSpec((top, tokens), lambda i, *_: (0, 0)),
                pl.BlockSpec((tokens, tile), lambda i, *_: (0, i)),
            ],
            out_specs=pl.BlockSpec((rows, tile), lambda i, *_: (0, i)),
            scratch_shapes=[pltpu.VMEM((rows, tokens), BF16)],
        ),
        compiler_params=params("arbitrary"),
        cost_estimate=pl.CostEstimate(flops=2 * rows * tokens * d, bytes_accessed=2 * (rows + tokens) * d, transcendentals=0),
        name="dispatch",
    )(rows_used, place, x)


def combine_matrix(place, gate, rows):
    sources, tokens, top = place.shape
    block = 128

    def kernel(place_ref, gate_ref, c_ref):
        column = lax.broadcasted_iota(I32, (block, rows), 1)
        total = jnp.zeros((block, rows), F32)
        for k in range(top):
            total = jnp.where(column == place_ref[0, :, k:k + 1], gate_ref[0, :, k:k + 1], total)
        c_ref[0] = total.astype(BF16)

    spec = pl.BlockSpec((1, block, top), lambda a, i: (a, i, 0))
    return pl.pallas_call(
        kernel,
        out_shape=jax.ShapeDtypeStruct((sources, tokens, rows), BF16),
        grid=(sources, tokens // block),
        in_specs=[spec, spec],
        out_specs=pl.BlockSpec((1, block, rows), lambda a, i: (a, i, 0)),
        compiler_params=params("arbitrary", "arbitrary"),
        cost_estimate=pl.CostEstimate(flops=sources * tokens * rows * top * 3, bytes_accessed=sources * tokens * rows * 2, transcendentals=0),
        name="combine_matrix",
    )(place, gate)


def up(count, source_at, expert_at, zs, w_gate, w_up, slots):
    experts, d, ff = w_gate.shape
    sources = len(zs)
    rows = sources * slots
    tile = 512
    sizes = list(range(64, rows + 1, 64))

    def kernel(count_ref, source_at_ref, expert_at_ref, *refs):
        z_refs, (wg_ref, wu_ref, h_ref, z_ref, sem) = refs[:sources], refs[sources:]
        e, f = pl.program_id(0), pl.program_id(1)

        def copies(e, act):
            slot = lax.rem(e, 2)
            for a in range(sources):
                for g in range(slots // GROUP):
                    @pl.when(g * GROUP < count_ref[a, e])
                    def _(a=a, g=g):
                        act(pltpu.make_async_copy(
                            z_refs[a].at[pl.ds(pl.multiple_of(source_at_ref[a, e] + g * GROUP, GROUP), GROUP), :],
                            z_ref.at[slot, pl.ds(pl.multiple_of(expert_at_ref[e, a] + g * GROUP, GROUP), GROUP), :],
                            sem.at[slot, a, g]))

        used = expert_at_ref[e, sources]

        @pl.when(f == 0)
        def _():
            @pl.when(e == 0)
            def _():
                copies(e, lambda c: c.start())

            copies(e, lambda c: c.wait())

            @pl.when(e + 1 < experts)
            def _():
                copies(e + 1, lambda c: c.start())

            z_ref[lax.rem(e, 2), pl.ds(pl.multiple_of(used, GROUP), 64), :] = jnp.zeros((64, d), BF16)

        for size in sizes:
            @pl.when((used > size - 64) & (used <= size))
            def _(size=size):
                z = z_ref[lax.rem(e, 2), :size, :]
                a = jnp.dot(z, wg_ref[0], preferred_element_type=F32)
                b = jnp.dot(z, wu_ref[0], preferred_element_type=F32)
                h_ref[0, :size, :] = (jax.nn.silu(a) * b).astype(BF16)

    weight = pl.BlockSpec((1, d, tile), lambda e, f, *_: (e, 0, f))
    return pl.pallas_call(
        kernel,
        out_shape=jax.ShapeDtypeStruct((experts, rows, ff), BF16),
        grid_spec=pltpu.PrefetchScalarGridSpec(
            num_scalar_prefetch=3,
            grid=(experts, ff // tile),
            in_specs=[ANY] * sources + [weight, weight],
            out_specs=pl.BlockSpec((1, rows, tile), lambda e, f, *_: (e, 0, f)),
            scratch_shapes=[
                pltpu.VMEM((2, rows + 64, d), BF16),
                pltpu.SemaphoreType.DMA((2, sources, slots // GROUP)),
            ],
        ),
        compiler_params=params("arbitrary", "arbitrary"),
        cost_estimate=pl.CostEstimate(
            flops=4 * experts * rows * d * ff, bytes_accessed=4 * experts * d * ff, transcendentals=experts * rows * ff),
        name="up",
    )(count, source_at, expert_at, *zs, w_gate, w_up)


def down(source_at, expert_at, h, w_down, c, first, width):
    experts, rows, ff = h.shape
    sources, tokens, columns = c.shape
    slots = rows // sources
    sizes = list(range(64, rows + 1, 64))
    depths = list(range(256, columns + 1, 256))
    tile = 256
    types = (F32, BF16, F32, BF16)

    def kernel(source_at_ref, expert_at_ref, h_ref, w_ref, c_ref, *refs):
        y_refs, (o_ref, out_ref) = refs[:sources], refs[sources:]
        e = pl.program_id(0)
        used = expert_at_ref[e, sources]

        @pl.when(e == 0)
        def _():
            o_ref[...] = jnp.zeros_like(o_ref)
            for a in range(sources):
                out_ref[a] = jnp.zeros(out_ref.shape[1:], BF16)

        for size in sizes:
            @pl.when((used > size - 64) & (used <= size))
            def _(size=size):
                o_ref[:size, :] = jnp.dot(h_ref[0, :size, :], w_ref[0], preferred_element_type=F32).astype(BF16)

        for a in range(sources):
            out_ref[a, pl.ds(pl.multiple_of(source_at_ref[a, e], GROUP), slots), :] = (
                o_ref[pl.ds(pl.multiple_of(expert_at_ref[e, a], GROUP), slots), :])

        @pl.when(e == experts - 1)
        def _():
            for a in range(sources):
                total = source_at_ref[a, experts]
                for depth in depths:
                    low = depth - 256 if depth > 256 else -1

                    @pl.when((total > low) & (total <= depth))
                    def _(a=a, depth=depth):
                        def part(i, _):
                            at = pl.ds(pl.multiple_of(i * tile, tile), tile)
                            y_refs[a][:, at] = jnp.dot(
                                c_ref[a, :, :depth], out_ref[a, :depth, at], preferred_element_type=F32).astype(types[a])
                            return 0

                        lax.fori_loop(0, width // tile, part, 0)

    step = first // width
    return pl.pallas_call(
        kernel,
        out_shape=[jax.ShapeDtypeStruct((tokens, width), t) for t in types],
        grid_spec=pltpu.PrefetchScalarGridSpec(
            num_scalar_prefetch=2,
            grid=(experts,),
            in_specs=[
                pl.BlockSpec((1, rows, ff), lambda e, *_: (e, 0, 0)),
                pl.BlockSpec((1, ff, width), lambda e, *_: (e, 0, step)),
                pl.BlockSpec((sources, tokens, columns), lambda e, *_: (0, 0, 0)),
            ],
            out_specs=[pl.BlockSpec((tokens, width), lambda e, *_: (0, 0))] * sources,
            scratch_shapes=[
                pltpu.VMEM((rows + slots, width), BF16),
                pltpu.VMEM((sources, columns + slots, width), BF16),
            ],
        ),
        compiler_params=params("arbitrary"),
        cost_estimate=pl.CostEstimate(
            flops=2 * experts * rows * ff * width, bytes_accessed=2 * experts * ff * width, transcendentals=0),
        name="down",
    )(source_at, expert_at, h, w_down, c)


def solution(mesh):
    members = mesh.shape["ep"]

    def swap(v, bit):
        return lax.ppermute(v, "ep", [(i, i ^ bit) for i in range(members)])

    def whole(x, expert, slot, gate, w_gate, w_up, w_down):
        tokens, top = expert.shape[2:]
        experts = w_gate.shape[0]
        slots = 5 * tokens * top // (4 * experts * members)
        rows = experts * slots
        x, expert, slot, gate = x[0, 0], expert[0, 0], slot[0, 0], gate[0, 0]

        routing = jnp.concatenate([
            expert.T.astype(F32), jnp.minimum(slot, slots).T.astype(F32), gate.T.astype(BF16).astype(F32)])
        near = swap(routing, 1)
        far = swap(routing, 2)
        across = swap(routing, 3)
        x1 = swap(x, 1)
        x2 = swap(x, 2)
        x3 = swap(x2, 1)

        routing = jnp.stack([routing, near, far, across])
        mine = routing[:, :top].astype(I32) - lax.axis_index("ep") * experts
        place = routing[:, top:2 * top].astype(I32)
        weight = routing[:, 2 * top:]
        kept = (mine >= 0) & (mine < experts) & (place < slots)
        mine = jnp.where(kept, mine, -1)
        is_at = mine[:, None] == jnp.arange(experts, dtype=I32)[None, :, None, None]
        count = jnp.max(jnp.where(is_at, place[:, None] + 1, 0), axis=(2, 3))
        size = (count + GROUP - 1) // GROUP * GROUP
        before = jnp.arange(experts + 1)[:, None] > jnp.arange(experts)[None, :]
        source_at = jnp.sum(jnp.where(before[None], size[:, None, :], 0), axis=2).astype(I32)
        before = jnp.arange(members + 1)[:, None] > jnp.arange(members)[None, :]
        expert_at = jnp.sum(jnp.where(before[None], size.T[:, None, :], 0), axis=2).astype(I32)
        shift = jnp.sum(jnp.where(is_at, source_at[:, :experts, None, None], 0), axis=1)
        place = jnp.where(kept, place + shift, -1)

        c = combine_matrix(place.swapaxes(1, 2), weight.swapaxes(1, 2), rows)
        zs = []
        for a, v in enumerate((x, x1, x2, x3)):
            zs.append(dispatch(source_at[a, experts:], place[a], v, rows))
        h = up(count, source_at, expert_at, zs, w_gate, w_up, slots)

        first, parts = 0, []
        for width in CHUNKS:
            own, near, far, across = down(source_at, expert_at, h, w_down, c, first, width)
            first += width
            met = (far + swap(across, 1).astype(F32)).astype(BF16)
            own = own + swap(near, 1).astype(F32)
            back = swap(met, 2)
            h, met = lax.optimization_barrier((h, met))
            parts.append((own, back))
        y = jnp.concatenate([(own + back.astype(F32)).astype(BF16) for own, back in parts], axis=1)
        return y[None, None]

    data, weights = P("dp", "ep"), P("ep")
    return jax.shard_map(
        whole, mesh=mesh, in_specs=(data,) * 4 + (weights,) * 3, out_specs=data, check_vma=False)
```

time: 1430 us -> 606 us (0.42)
  blocking collectives: 475 us -> 0 us
  matrix products: 469 us -> 0 us
  Pallas kernels: 0 us -> 399 us
  waiting for transfers between devices: 443 us -> 153 us
  other arithmetic: 0.01 us -> 25.1 us
  local copies, waits for them, and re-layouts: 29.9 us -> 11.5 us
    another operation x1 -> x0, blocking collectives: 475 us -> none  [placed(): return lax.with_sharding_constraint(v, NamedSharding(mesh, P(*spec)))]
    dot_general x7 -> x0, matrix products: 469 us -> none  [einsum(): return jnp.einsum(form, a.astype(jnp.float32), b.astype(jnp.float32))]
    another operation x1 -> x0, waiting for transfers between devices: 443 us -> none  [placed(): return lax.with_sharding_constraint(v, NamedSharding(mesh, P(*spec)))]
    pallas_call x0 -> x11, Pallas kernels: none -> 399 us  [the longest x5 178 us: down(): pl.pallas_call(kernel, out_shape=[jax.ShapeDtypeStruct((tokens, width), t...]
    ppermute x0 -> x21, waiting for transfers between devices: none -> 153 us  [swap(): return lax.ppermute(v, 'ep', [(i, i ^ bit) for i in range(members)])]
    another operation x1 -> x0, local copies, waits for them, and re-layouts: 28 us -> none  [placed(): return lax.with_sharding_constraint(v, NamedSharding(mesh, P(*spec)))]
  transfers between devices with their start and end apart: 1 -> 21, of which waited for: 1 -> 9; matrix products, arithmetic and copies ran while one was open for 1% -> 5% of each run, Pallas kernels for 0% -> 18%
where the time goes in v1:
time: 606 us; the launch traced here: 600 us
  Pallas kernels  399 us (66%)
  waiting for transfers between devices  153 us (25%)
  other arithmetic  25.1 us (4%)
  local copies, waits for them, and re-layouts  11.5 us (2%)
  starting transfers between devices  11.2 us (2%)
    pallas_call x5, Pallas kernels, down(): pl.pallas_call(kernel, out_shape=[jax.ShapeDtypeStruct((tokens, width), t...  178 us
    pallas_call x1, Pallas kernels, up(): pl.pallas_call(kernel, out_shape=jax.ShapeDtypeStruct((experts, rows, ff)...  155 us
    ppermute x21, waiting for transfers between devices, swap(): return lax.ppermute(v, 'ep', [(i, i ^ bit) for i in range(members)])  153 us
    pallas_call x4, Pallas kernels, dispatch(): pl.pallas_call(kernel, out_shape=jax.ShapeDtypeStruct((rows, d), BF16), g...  48.3 us
    pallas_call x1, Pallas kernels, combine_matrix(): pl.pallas_call(kernel, out_shape=jax.ShapeDtypeStruct((sources, tokens, r...  18.1 us
  transfers between devices with their start and end apart: 21, of which 9 were waited for; matrix products, arithmetic and copies ran while one was open for 5% of the time, Pallas kernels for 18%

profile of v1, /device:TPU:0, one launch (start us, length us, event | category | flops | bytes accessed | tf_op | source)
XLA Modules:
  0.0 600.5 jit_solution(10777944297365183613)
XLA Ops:
  0.0 3.3 collective-permute-start.4
  4.1 90.1 %collective-permute-done.4.x_ref = bf16[512,4096]{1,0:T(8,128)(2,1)} collective-permute-done((bf16[512,4096]{1,0:T(8,128)(2,1)}, bf16[512,4096]{1,0:T(8,128)(2,1)}, u32[]{:S(2)}, u32[]{:S(2)}) %collective-permute-start.4) | collective-permute-done | bytes 4194336 | tf_op jit(solution)/shard_map/ppermute | solution.py:230
  97.2 4.5 collective-permute-done
  115.2 18.1 %combine_matrix.1.c_ref = bf16[4,512,1280]{2,1,0:T(8,128)(2,1)} custom-call(s32[4,512,8]{2,1,0:T(8,128)} %bitcast.51, f32[4,512,8]{2,1,0:T(8,128)} %bitcast.52), custom_call_target="tpu_custom_call" | custom-call | flops 62914560 | bytes 5242880 | tf_op jit(solution)/shard_map/combine_matrix/pallas_call | solution.py:76
  133.8 12.1 %dispatch.4.refs_0_ = bf16[1280,4096]{1,0:T(8,128)(2,1)} custom-call(s32[1]{0:T(128)} %bitcast.11.used_ref, s32[8,512]{1,0:T(8,128)} %copy.50.place_ref, bf16[512,4096]{1,0:T(8,128)(2,1)} %bitcast.59), custom_call_target="tpu_custom_call" | custom-call | flops 5368709120 | bytes 14680064 | tf_op jit(solution)/shard_map/dispatch/pallas_call | solution.py:45
  145.9 12.2 %dispatch.6.refs_2_ = bf16[1280,4096]{1,0:T(8,128)(2,1)} custom-call(s32[1]{0:T(128)} %bitcast.16.used_ref, s32[8,512]{1,0:T(8,128)} %copy.52.place_ref, bf16[512,4096]{1,0:T(8,128)(2,1)} %collective-permute-done.4.x_ref), custom_call_target="tpu_custom_call" | custom-call | flops 5368709120 | bytes 14680064 | tf_op jit(solution)/shard_map/dispatch/pallas_call | solution.py:45
  158.1 12.0 %dispatch.5.refs_1_ = bf16[1280,4096]{1,0:T(8,128)(2,1)} custom-call(s32[1]{0:T(128)} %bitcast.14.used_ref, s32[8,512]{1,0:T(8,128)} %copy.51.place_ref, bf16[512,4096]{1,0:T(8,128)(2,1)} %collective-permute-done.3.x_ref), custom_call_target="tpu_custom_call" | custom-call | flops 5368709120 | bytes 14680064 | tf_op jit(solution)/shard_map/dispatch/pallas_call | solution.py:45
  170.0 12.1 %dispatch.7.refs_3_ = bf16[1280,4096]{1,0:T(8,128)(2,1)} custom-call(s32[1]{0:T(128)} %bitcast.18.used_ref, s32[8,512]{1,0:T(8,128)} %copy.53.place_ref, bf16[512,4096]{1,0:T(8,128)(2,1)} %collective-permute-done.5.x_ref), custom_call_target="tpu_custom_call" | custom-call | flops 5368709120 | bytes 14680064 | tf_op jit(solution)/shard_map/dispatch/pallas_call | solution.py:45
  182.1 155.2 %up.1.h_ref = bf16[16,320,1536]{2,1,0:T(8,128)(2,1)} custom-call(s32[4,16]{1,0:T(4,128)} %copy-done.9, s32[4,17]{1,0:T(4,128)} %copy-done.8, s32[16,5]{1,0:T(8,128)} %copy.56.expert_at_ref, bf16[1280,4096]{1,0:T(8,128)(2,1)} %dispatch.4.refs_0_, bf16[1280,4096]{1,0:T(8,128)(2,1)} %dispatch.5.refs_1_, bf16[1280,4096]{1,0:T(8,128)(2,1)} %dispatch.6.refs_2_, ...), custom_call_target="tpu_custom_call" | custom-call | flops 128849018880 | bytes 402653184 | tf_op jit(solution)/shard_map/up/pallas_call | solution.py:135
  337.3 40.8 %down.5 = (f32[512,1024]{1,0:T(8,128)}, bf16[512,1024]{1,0:T(8,128)(2,1)}, f32[512,1024]{1,0:T(8,128)}, bf16[512,1024]{1,0:T(8,128)(2,1)}) custom-call(s32[4,17]{1,0:T(4,128)} %copy-done.8, s32[16,5]{1,0:T(8,128)} %copy.56.expert_at_ref, bf16[16,320,1536]{2,1,0:T(8,128)(2,1)} %up.1.h_ref, bf16[16,1536,4096]{2,1,0:T(8,128)(2,1)} %w_ref.9, ...), custom_call_target="tpu_custom_call" | custom-call | flops 16106127360 | bytes 50331648 | tf_op jit(solution)/shard_map/down/pallas_call | solution.py:202
  378.1 2.9 collective-permute-done.7
  381.0 2.9 add_convert_fusion.5
  383.9 40.6 %down.6 = (f32[512,1024]{1,0:T(8,128)}, bf16[512,1024]{1,0:T(8,128)(2,1)}, f32[512,1024]{1,0:T(8,128)}, bf16[512,1024]{1,0:T(8,128)(2,1)}) custom-call(s32[4,17]{1,0:T(4,128)} %copy-done.8, s32[16,5]{1,0:T(8,128)} %copy.56.expert_at_ref, bf16[16,320,1536]{2,1,0:T(8,128)(2,1)} %up.1.h_ref, bf16[16,1536,4096]{2,1,0:T(8,128)(2,1)} %w_ref.9, ...), custom_call_target="tpu_custom_call" | custom-call | flops 16106127360 | bytes 50331648 | tf_op jit(solution)/shard_map/down/pallas_call | solution.py:202
  424.5 2.9 collective-permute-done.10
  427.4 3.0 add_convert_fusion.3
  430.4 40.5 %down.7 = (f32[512,1024]{1,0:T(8,128)}, bf16[512,1024]{1,0:T(8,128)(2,1)}, f32[512,1024]{1,0:T(8,128)}, bf16[512,1024]{1,0:T(8,128)(2,1)}) custom-call(s32[4,17]{1,0:T(4,128)} %copy-done.8, s32[16,5]{1,0:T(8,128)} %copy.56.expert_at_ref, bf16[16,320,1536]{2,1,0:T(8,128)(2,1)} %up.1.h_ref, bf16[16,1536,4096]{2,1,0:T(8,128)(2,1)} %w_ref.9, ...), custom_call_target="tpu_custom_call" | custom-call | flops 16106127360 | bytes 50331648 | tf_op jit(solution)/shard_map/down/pallas_call | solution.py:202
  473.8 3.0 add_convert_fusion.1
  476.8 28.0 %down.8 = (f32[512,512]{1,0:T(8,128)}, bf16[512,512]{1,0:T(8,128)(2,1)}, f32[512,512]{1,0:T(8,128)}, bf16[512,512]{1,0:T(8,128)(2,1)}) custom-call(s32[4,17]{1,0:T(4,128)} %copy-done.8, s32[16,5]{1,0:T(8,128)} %copy.56.expert_at_ref, bf16[16,320,1536]{2,1,0:T(8,128)(2,1)} %up.1.h_ref, bf16[16,1536,4096]{2,1,0:T(8,128)(2,1)} %w_ref.9, ...), custom_call_target="tpu_custom_call" | custom-call | flops 8053063680 | bytes 25165824 | tf_op jit(solution)/shard_map/down/pallas_call | solution.py:202
  509.5 28.1 %down.9 = (f32[512,512]{1,0:T(8,128)}, bf16[512,512]{1,0:T(8,128)(2,1)}, f32[512,512]{1,0:T(8,128)}, bf16[512,512]{1,0:T(8,128)(2,1)}) custom-call(s32[4,17]{1,0:T(4,128)} %copy-done.8, s32[16,5]{1,0:T(8,128)} %copy.56.expert_at_ref, bf16[16,320,1536]{2,1,0:T(8,128)(2,1)} %up.1.h_ref, bf16[16,1536,4096]{2,1,0:T(8,128)(2,1)} %w_ref.9, ...), custom_call_target="tpu_custom_call" | custom-call | flops 8053063680 | bytes 25165824 | tf_op jit(solution)/shard_map/down/pallas_call | solution.py:202
  537.6 2.8 fusion
  541.0 12.6 %collective-permute-done.11 = bf16[512,1024]{1,0:T(8,128)(2,1)} collective-permute-done((bf16[512,1024]{1,0:T(8,128)(2,1)}, bf16[512,1024]{1,0:T(8,128)(2,1)}, u32[]{:S(2)}, u32[]{:S(2)}) %collective-permute-start.11) | collective-permute-done | bytes 1048608 | tf_op jit(solution)/shard_map/ppermute | solution.py:230
  558.2 17.9 %collective-permute-done.14 = bf16[512,1024]{1,0:T(8,128)(2,1)} collective-permute-done((bf16[512,1024]{1,0:T(8,128)(2,1)}, bf16[512,1024]{1,0:T(8,128)(2,1)}, u32[]{:S(2)}, u32[]{:S(2)}) %collective-permute-start.14) | collective-permute-done | bytes 1048608 | tf_op jit(solution)/shard_map/ppermute | solution.py:230
  578.3 8.9 %collective-permute-done.17 = bf16[512,512]{1,0:T(8,128)(2,1)S(1)} collective-permute-done((bf16[512,512]{1,0:T(8,128)(2,1)S(1)}, bf16[512,512]{1,0:T(8,128)(2,1)S(1)}, u32[]{:S(2)}, u32[]{:S(2)}) %collective-permute-start.17) | collective-permute-done | bytes 524320 | tf_op jit(solution)/shard_map/ppermute | solution.py:230
  587.4 10.5 %collective-permute-done.20 = bf16[512,512]{1,0:T(8,128)(2,1)S(1)} collective-permute-done((bf16[512,512]{1,0:T(8,128)(2,1)S(1)}, bf16[512,512]{1,0:T(8,128)(2,1)S(1)}, u32[]{:S(2)}, u32[]{:S(2)}) %collective-permute-start.20) | collective-permute-done | bytes 524320 | tf_op jit(solution)/shard_map/ppermute | solution.py:230
  (91 shorter events, 35.1 us)
Async XLA Ops:
  0.0 94.2 %collective-permute-start.4 = (bf16[512,4096]{1,0:T(8,128)(2,1)}, bf16[512,4096]{1,0:T(8,128)(2,1)}, u32[]{:S(2)}, u32[]{:S(2)}) collective-permute-start(bf16[512,4096]{1,0:T(8,128)(2,1)} %bitcast.57), channel_id=1, source_target_pairs={{0,2},{1,3},{2,0},{3,1},{4,6},{5,7},{6,4},{7,5}} | collective-permute-start | bytes 12582920 | tf_op jit(solution)/shard_map/ppermute | solution.py:230
  3.3 154.7 %collective-permute-start.3 = (bf16[512,4096]{1,0:T(8,128)(2,1)}, bf16[512,4096]{1,0:T(8,128)(2,1)}, u32[]{:S(2)}, u32[]{:S(2)}) collective-permute-start(bf16[512,4096]{1,0:T(8,128)(2,1)} %bitcast.58), channel_id=1, source_target_pairs={{0,1},{1,0},{2,3},{3,2},{4,5},{5,4},{6,7},{7,6}} | collective-permute-start | bytes 12582920 | tf_op jit(solution)/shard_map/ppermute | solution.py:230
  94.2 75.8 %collective-permute-start.5 = (bf16[512,4096]{1,0:T(8,128)(2,1)}, bf16[512,4096]{1,0:T(8,128)(2,1)}, u32[]{:S(2)}, u32[]{:S(2)}) collective-permute-start(bf16[512,4096]{1,0:T(8,128)(2,1)} %collective-permute-done.4.x_ref), channel_id=1, source_target_pairs={{0,1},{1,0},{2,3},{3,2},{4,5},{5,4},{6,7},{7,6}} | collective-permute-start | bytes 12582920 | tf_op jit(solution)/shard_map/ppermute | solution.py:230
  94.9 6.8 %collective-permute-start = (f32[24,512]{1,0:T(8,128)S(1)}, f32[24,512]{1,0:T(8,128)S(1)}, u32[]{:S(2)}, u32[]{:S(2)}) collective-permute-start(f32[24,512]{1,0:T(8,128)S(1)} %get-tuple-element.63), channel_id=1, source_target_pairs={{0,1},{1,0},{2,3},{3,2},{4,5},{5,4},{6,7},{7,6}} | collective-permute-start | bytes 147464 | tf_op jit(solution)/shard_map/ppermute | solution.py:230
  95.5 6.2 %collective-permute-start.1 = (f32[24,512]{1,0:T(8,128)S(1)}, f32[24,512]{1,0:T(8,128)S(1)}, u32[]{:S(2)}, u32[]{:S(2)}) collective-permute-start(f32[24,512]{1,0:T(8,128)S(1)} %get-tuple-element.63), channel_id=1, source_target_pairs={{0,2},{1,3},{2,0},{3,1},{4,6},{5,7},{6,4},{7,5}} | collective-permute-start | bytes 147464 | tf_op jit(solution)/shard_map/ppermute | solution.py:230
  97.2 4.5 collective-permute-start.2
  106.9 26.3 %copy-start.8 = (s32[4,17]{1,0:T(4,128)}, s32[4,17]{1,0:T(4,128)S(1)}, u32[]{:S(2)}) copy-start(s32[4,17]{1,0:T(4,128)S(1)} %select_reduce_fusion.2.source_at_ref) | copy-start | bytes 820
  378.1 2.9 collective-permute-start.7
  424.5 2.9 collective-permute-start.10
  470.9 2.9 collective-permute-start.13
  470.9 38.3 %collective-permute-start.6 = (bf16[512,1024]{1,0:T(8,128)(2,1)}, bf16[512,1024]{1,0:T(8,128)(2,1)}, u32[]{:S(2)}, u32[]{:S(2)}) collective-permute-start(bf16[512,1024]{1,0:T(8,128)(2,1)} %get-tuple-element.30), channel_id=1, source_target_pairs={{0,1},{1,0},{2,3},{3,2},{4,5},{5,4},{6,7},{7,6}} | collective-permute-start | bytes 3145736 | tf_op jit(solution)/shard_map/ppermute | solution.py:230
  504.8 2.3 collective-permute-start.16
  504.8 32.8 %collective-permute-start.8 = (bf16[512,1024]{1,0:T(8,128)(2,1)}, bf16[512,1024]{1,0:T(8,128)(2,1)}, u32[]{:S(2)}, u32[]{:S(2)}) collective-permute-start(bf16[512,1024]{1,0:T(8,128)(2,1)} %add_convert_fusion.5), channel_id=1, source_target_pairs={{0,2},{1,3},{2,0},{3,1},{4,6},{5,7},{6,4},{7,5}} | collective-permute-start | bytes 3145736 | tf_op jit(solution)/shard_map/ppermute | solution.py:230
  504.8 35.7 %collective-permute-start.9 = (bf16[512,1024]{1,0:T(8,128)(2,1)}, bf16[512,1024]{1,0:T(8,128)(2,1)}, u32[]{:S(2)}, u32[]{:S(2)}) collective-permute-start(bf16[512,1024]{1,0:T(8,128)(2,1)} %get-tuple-element.35), channel_id=1, source_target_pairs={{0,1},{1,0},{2,3},{3,2},{4,5},{5,4},{6,7},{7,6}} | collective-permute-start | bytes 3145736 | tf_op jit(solution)/shard_map/ppermute | solution.py:230
  505.3 48.3 %collective-permute-start.11 = (bf16[512,1024]{1,0:T(8,128)(2,1)}, bf16[512,1024]{1,0:T(8,128)(2,1)}, u32[]{:S(2)}, u32[]{:S(2)}) collective-permute-start(bf16[512,1024]{1,0:T(8,128)(2,1)} %add_convert_fusion.3), channel_id=1, source_target_pairs={{0,2},{1,3},{2,0},{3,1},{4,6},{5,7},{6,4},{7,5}} | collective-permute-start | bytes 3145736 | tf_op jit(solution)/shard_map/ppermute | solution.py:230
  507.0 49.1 %collective-permute-start.12 = (bf16[512,1024]{1,0:T(8,128)(2,1)}, bf16[512,1024]{1,0:T(8,128)(2,1)}, u32[]{:S(2)}, u32[]{:S(2)}) collective-permute-start(bf16[512,1024]{1,0:T(8,128)(2,1)} %get-tuple-element.40), channel_id=1, source_target_pairs={{0,1},{1,0},{2,3},{3,2},{4,5},{5,4},{6,7},{7,6}} | collective-permute-start | bytes 3145736 | tf_op jit(solution)/shard_map/ppermute | solution.py:230
  509.2 66.8 %collective-permute-start.14 = (bf16[512,1024]{1,0:T(8,128)(2,1)}, bf16[512,1024]{1,0:T(8,128)(2,1)}, u32[]{:S(2)}, u32[]{:S(2)}) collective-permute-start(bf16[512,1024]{1,0:T(8,128)(2,1)} %add_convert_fusion.1), channel_id=1, source_target_pairs={{0,2},{1,3},{2,0},{3,1},{4,6},{5,7},{6,4},{7,5}} | collective-permute-start | bytes 3145736 | tf_op jit(solution)/shard_map/ppermute | solution.py:230
  537.6 18.3 %collective-permute-start.19 = (bf16[512,512]{1,0:T(8,128)(2,1)}, bf16[512,512]{1,0:T(8,128)(2,1)S(1)}, u32[]{:S(2)}, u32[]{:S(2)}) collective-permute-start(bf16[512,512]{1,0:T(8,128)(2,1)} %get-tuple-element.52), channel_id=1, source_target_pairs={{0,1},{1,0},{2,3},{3,2},{4,5},{5,4},{6,7},{7,6}} | collective-permute-start | bytes 1572872 | tf_op jit(solution)/shard_map/ppermute | solution.py:230
  540.5 37.8 %collective-permute-start.15 = (bf16[512,512]{1,0:T(8,128)(2,1)S(1)}, bf16[512,512]{1,0:T(8,128)(2,1)S(1)}, u32[]{:S(2)}, u32[]{:S(2)}) collective-permute-start(bf16[512,512]{1,0:T(8,128)(2,1)S(1)} %copy-done.10), channel_id=1, source_target_pairs={{0,1},{1,0},{2,3},{3,2},{4,5},{5,4},{6,7},{7,6}} | collective-permute-start | bytes 1572872 | tf_op jit(solution)/shard_map/ppermute | solution.py:230
  555.9 20.2 %copy-start.1 = (f32[512,1024]{1,0:T(8,128)S(1)}, f32[512,1024]{1,0:T(8,128)}, u32[]{:S(2)}) copy-start(f32[512,1024]{1,0:T(8,128)} %get-tuple-element.39) | copy-start | bytes 6291460
  555.9 31.3 %collective-permute-start.17 = (bf16[512,512]{1,0:T(8,128)(2,1)S(1)}, bf16[512,512]{1,0:T(8,128)(2,1)S(1)}, u32[]{:S(2)}, u32[]{:S(2)}) collective-permute-start(bf16[512,512]{1,0:T(8,128)(2,1)S(1)} %copy-done.6), channel_id=1, source_target_pairs={{0,2},{1,3},{2,0},{3,1},{4,6},{5,7},{6,4},{7,5}} | collective-permute-start | bytes 1572872 | tf_op jit(solution)/shard_map/ppermute | solution.py:230
  556.0 31.5 %collective-permute-start.18 = (bf16[512,512]{1,0:T(8,128)(2,1)S(1)}, bf16[512,512]{1,0:T(8,128)(2,1)S(1)}, u32[]{:S(2)}, u32[]{:S(2)}) collective-permute-start(bf16[512,512]{1,0:T(8,128)(2,1)S(1)} %copy-done.11), channel_id=1, source_target_pairs={{0,1},{1,0},{2,3},{3,2},{4,5},{5,4},{6,7},{7,6}} | collective-permute-start | bytes 1572872 | tf_op jit(solution)/shard_map/ppermute | solution.py:230
  556.2 41.8 %collective-permute-start.20 = (bf16[512,512]{1,0:T(8,128)(2,1)S(1)}, bf16[512,512]{1,0:T(8,128)(2,1)S(1)}, u32[]{:S(2)}, u32[]{:S(2)}) collective-permute-start(bf16[512,512]{1,0:T(8,128)(2,1)S(1)} %add_convert_fusion.7), channel_id=1, source_target_pairs={{0,2},{1,3},{2,0},{3,1},{4,6},{5,7},{6,4},{7,5}} | collective-permute-start | bytes 1572872 | tf_op jit(solution)/shard_map/ppermute | solution.py:230
  578.3 19.7 %copy-start.4 = (f32[512,512]{1,0:T(8,128)S(1)}, f32[512,512]{1,0:T(8,128)}, u32[]{:S(2)}) copy-start(f32[512,512]{1,0:T(8,128)} %get-tuple-element.49) | copy-start | bytes 3145732
  (9 other events, 50.5 us)

commit v2 on v1

--- a/solution.py
+++ b/solution.py
@@ -8,7 +8,6 @@
 F32, BF16, I32 = jnp.float32, jnp.bfloat16, jnp.int32
 VMEM_LIMIT = 64 * 1024 * 1024 - 64 * 1024 * 2
 GROUP = 16
-CHUNKS = (1024, 1024, 1024, 512, 512)
 ANY = pl.BlockSpec(memory_space=pl.ANY)
 
 
@@ -93,7 +92,7 @@
     sizes = list(range(64, rows + 1, 64))
 
     def kernel(count_ref, source_at_ref, expert_at_ref, *refs):
-        z_refs, (wg_ref, wu_ref, h_ref, z_ref, sem) = refs[:sources], refs[sources:]
+        z_refs, (wg_ref, wu_ref, h_ref, z_ref, hs_ref, sem) = refs[:sources], refs[sources:]
         e, f = pl.program_id(0), pl.program_id(1)
 
         def copies(e, act):
@@ -129,7 +128,11 @@
                 z = z_ref[lax.rem(e, 2), :size, :]
                 a = jnp.dot(z, wg_ref[0], preferred_element_type=F32)
                 b = jnp.dot(z, wu_ref[0], preferred_element_type=F32)
-                h_ref[0, :size, :] = (jax.nn.silu(a) * b).astype(BF16)
+                hs_ref[:size, :] = (jax.nn.silu(a) * b).astype(BF16)
+
+        hs_ref[pl.ds(pl.multiple_of(used, GROUP), slots), :] = jnp.zeros((slots, tile), BF16)
+        for a in range(sources):
+            h_ref[0, a * slots:(a + 1) * slots, :] = hs_ref[pl.ds(pl.multiple_of(expert_at_ref[e, a], GROUP), slots), :]
 
     weight = pl.BlockSpec((1, d, tile), lambda e, f, *_: (e, 0, f))
     return pl.pallas_call(
@@ -142,6 +145,7 @@
             out_specs=pl.BlockSpec((1, rows, tile), lambda e, f, *_: (e, 0, f)),
             scratch_shapes=[
                 pltpu.VMEM((2, rows + 64, d), BF16),
+                pltpu.VMEM((rows + slots, tile), BF16),
                 pltpu.SemaphoreType.DMA((2, sources, slots // GROUP)),
             ],
         ),
@@ -152,75 +156,150 @@
     )(count, source_at, expert_at, *zs, w_gate, w_up)
 
 
-def down(source_at, expert_at, h, w_down, c, first, width):
+def finish(h, w_down, c):
     experts, rows, ff = h.shape
     sources, tokens, columns = c.shape
+    d = w_down.shape[2]
     slots = rows // sources
-    sizes = list(range(64, rows + 1, 64))
-    depths = list(range(256, columns + 1, 256))
-    tile = 256
-    types = (F32, BF16, F32, BF16)
-
-    def kernel(source_at_ref, expert_at_ref, h_ref, w_ref, c_ref, *refs):
-        y_refs, (o_ref, out_ref) = refs[:sources], refs[sources:]
-        e = pl.program_id(0)
-        used = expert_at_ref[e, sources]
-
-        @pl.when(e == 0)
-        def _():
-            o_ref[...] = jnp.zeros_like(o_ref)
+    width, batch, lag = 512, 4, 2
+    chunks, groups = d // width, experts // batch
+    block = (tokens, width)
+
+    def kernel(h_hbm, w_ref, c_hbm, y_hbm, h_ref, c_ref, out_ref, got3, got1, met, send3, send1, send2, far, own, y_ref,
+               h_sem, c_sem, y_sem, send3_sem, send1_sem, send2_sem, got3_sem, got1_sem, met_sem):
+        chunk, group = pl.program_id(0), pl.program_id(1)
+        me = lax.axis_index("ep")
+        beside = me + 1 - 2 * lax.rem(me, 2)
+        across = lax.rem(me + 2, 4)
+        half = lax.rem(chunk, 2)
+
+        def load_h(g):
+            at = pl.ds(pl.multiple_of(g * batch, batch), batch)
+            return pltpu.make_async_copy(h_hbm.at[at], h_ref.at[at], h_sem.at[g])
+
+        load_c = pltpu.make_async_copy(c_hbm, c_ref, c_sem)
+
+        def remote(source, target, slot, sent, got, number, to):
+            return pltpu.make_async_remote_copy(
+                src_ref=source.at[slot], dst_ref=target.at[number], send_sem=sent.at[slot], recv_sem=got.at[number],
+                device_id={"ep": to}, device_id_type=pl.DeviceIdType.MESH)
+
+        def to_beside3(n):
+            return remote(send3, got3, lax.rem(n, 2), send3_sem, got3_sem, n, beside)
+
+        def to_beside1(n):
+            return remote(send1, got1, lax.rem(n, 2), send1_sem, got1_sem, n, beside)
+
+        def to_across(n):
+            return remote(send2, met, lax.rem(n, 2), send2_sem, met_sem, n, across)
+
+        def write(n):
+            return pltpu.make_async_copy(
+                y_ref.at[lax.rem(n, 2)], y_hbm.at[:, pl.ds(pl.multiple_of(n * width, width), width)], y_sem.at[lax.rem(n, 2)])
+
+        @pl.when((chunk == 0) & (group == 0))
+        def _():
+            for g in range(groups):
+                load_h(g).start()
+            load_c.start()
+            barrier = pltpu.get_barrier_semaphore()
+            for to in (beside, across):
+                pl.semaphore_signal(barrier, inc=1, device_id={"ep": to}, device_id_type=pl.DeviceIdType.MESH)
+            pl.semaphore_wait(barrier, 2)
+
+        @pl.when(chunk == 0)
+        def _():
+            load_h(group).wait()
+
+        def expert(i, _):
+            e = group * batch + i
+            o = jnp.dot(h_ref[e], w_ref[i], preferred_element_type=F32).astype(BF16)
             for a in range(sources):
-                out_ref[a] = jnp.zeros(out_ref.shape[1:], BF16)
-
-        for size in sizes:
-            @pl.when((used > size - 64) & (used <= size))
-            def _(size=size):
-                o_ref[:size, :] = jnp.dot(h_ref[0, :size, :], w_ref[0], preferred_element_type=F32).astype(BF16)
-
-        for a in range(sources):
-            out_ref[a, pl.ds(pl.multiple_of(source_at_ref[a, e], GROUP), slots), :] = (
-                o_ref[pl.ds(pl.multiple_of(expert_at_ref[e, a], GROUP), slots), :])
-
-        @pl.when(e == experts - 1)
-        def _():
-            for a in range(sources):
-                total = source_at_ref[a, experts]
-                for depth in depths:
-                    low = depth - 256 if depth > 256 else -1
-
-                    @pl.when((total > low) & (total <= depth))
-                    def _(a=a, depth=depth):
-                        def part(i, _):
-                            at = pl.ds(pl.multiple_of(i * tile, tile), tile)
-                            y_refs[a][:, at] = jnp.dot(
-                                c_ref[a, :, :depth], out_ref[a, :depth, at], preferred_element_type=F32).astype(types[a])
-                            return 0
-
-                        lax.fori_loop(0, width // tile, part, 0)
-
-    step = first // width
+                out_ref[a, pl.ds(pl.multiple_of(e * slots, GROUP), slots), :] = o[a * slots:(a + 1) * slots]
+            return 0
+
+        lax.fori_loop(0, batch, expert, 0)
+
+        @pl.when(group == groups - 1)
+        def _():
+            @pl.when(chunk == 0)
+            def _():
+                load_c.wait()
+
+            @pl.when(chunk >= 2)
+            def _():
+                to_beside3(chunk - 2).wait_send()
+                to_beside1(chunk - 2).wait_send()
+                to_across(chunk - 2).wait_send()
+
+            def share(a):
+                return jnp.dot(c_ref[a], out_ref[a], preferred_element_type=F32)
+
+            send3[half] = share(3).astype(BF16)
+            send1[half] = share(1).astype(BF16)
+            to_beside3(chunk).start()
+            far[...] = share(2)
+            to_beside1(chunk).start()
+            own[lax.rem(chunk, lag + 1)] = share(0)
+            to_beside3(chunk).wait_recv()
+            send2[half] = (far[...] + got3[chunk].astype(F32)).astype(BF16)
+
+            def close(n):
+                to_beside1(n).wait_recv()
+                to_across(n).wait_recv()
+
+                @pl.when(n >= 2)
+                def _():
+                    write(n - 2).wait()
+
+                y_ref[lax.rem(n, 2)] = (
+                    own[lax.rem(n, lag + 1)] + got1[n].astype(F32) + met[n].astype(F32)).astype(BF16)
+                write(n).start()
+
+            to_across(chunk).start()
+
+            @pl.when(chunk >= lag)
+            def _():
+                close(chunk - lag)
+
+            @pl.when(chunk == chunks - 1)
+            def _():
+                for n in range(chunks - lag, chunks):
+                    close(n)
+                for n in range(chunks - 2, chunks):
+                    to_beside3(n).wait_send()
+                    to_beside1(n).wait_send()
+                    to_across(n).wait_send()
+                    write(n).wait()
+
+    dma = pltpu.SemaphoreType.DMA
     return pl.pallas_call(
         kernel,
-        out_shape=[jax.ShapeDtypeStruct((tokens, width), t) for t in types],
-        grid_spec=pltpu.PrefetchScalarGridSpec(
-            num_scalar_prefetch=2,
-            grid=(experts,),
-            in_specs=[
-                pl.BlockSpec((1, rows, ff), lambda e, *_: (e, 0, 0)),
-                pl.BlockSpec((1, ff, width), lambda e, *_: (e, 0, step)),
-                pl.BlockSpec((sources, tokens, columns), lambda e, *_: (0, 0, 0)),
-            ],
-            out_specs=[pl.BlockSpec((tokens, width), lambda e, *_: (0, 0))] * sources,
-            scratch_shapes=[
-                pltpu.VMEM((rows + slots, width), BF16),
-                pltpu.VMEM((sources, columns + slots, width), BF16),
-            ],
-        ),
-        compiler_params=params("arbitrary"),
+        out_shape=jax.ShapeDtypeStruct((tokens, d), BF16),
+        grid=(chunks, groups),
+        in_specs=[ANY, pl.BlockSpec((batch, ff, width), lambda n, g: (g, 0, n)), ANY],
+        out_specs=ANY,
+        scratch_shapes=[
+            pltpu.VMEM((experts, rows, ff), BF16),
+            pltpu.VMEM((sources, tokens, columns), BF16),
+            pltpu.VMEM((sources, columns, width), BF16),
+            pltpu.VMEM((chunks, *block), BF16),
+            pltpu.VMEM((chunks, *block), BF16),
+            pltpu.VMEM((chunks, *block), BF16),
+            pltpu.VMEM((2, *block), BF16),
+            pltpu.VMEM((2, *block), BF16),
+            pltpu.VMEM((2, *block), BF16),
+            pltpu.VMEM(block, F32),
+            pltpu.VMEM((lag + 1, *block), F32),
+            pltpu.VMEM((2, *block), BF16),
+            dma((groups,)), dma, dma((2,)), dma((2,)), dma((2,)), dma((2,)), dma((chunks,)), dma((chunks,)), dma((chunks,)),
+        ],
+        compiler_params=pltpu.CompilerParams(
+            dimension_semantics=("arbitrary", "arbitrary"), vmem_limit_bytes=VMEM_LIMIT, collective_id=0, has_side_effects=True),
         cost_estimate=pl.CostEstimate(
-            flops=2 * experts * rows * ff * width, bytes_accessed=2 * experts * ff * width, transcendentals=0),
-        name="down",
-    )(source_at, expert_at, h, w_down, c)
+            flops=2 * experts * rows * ff * d, bytes_accessed=2 * experts * ff * d, transcendentals=0),
+        name="finish",
+    )(h, w_down, c)
 
 
 def solution(mesh):
@@ -259,24 +338,16 @@
         before = jnp.arange(members + 1)[:, None] > jnp.arange(members)[None, :]
         expert_at = jnp.sum(jnp.where(before[None], size.T[:, None, :], 0), axis=2).astype(I32)
         shift = jnp.sum(jnp.where(is_at, source_at[:, :experts, None, None], 0), axis=1)
+        fixed = jnp.where(kept, place + mine * slots, -1)
         place = jnp.where(kept, place + shift, -1)
 
-        c = combine_matrix(place.swapaxes(1, 2), weight.swapaxes(1, 2), rows)
+        c = combine_matrix(fixed.swapaxes(1, 2), weight.swapaxes(1, 2), rows)
         zs = []
         for a, v in enumerate((x, x1, x2, x3)):
             zs.append(dispatch(source_at[a, experts:], place[a], v, rows))
         h = up(count, source_at, expert_at, zs, w_gate, w_up, slots)
 
-        first, parts = 0, []
-        for width in CHUNKS:
-            own, near, far, across = down(source_at, expert_at, h, w_down, c, first, width)
-            first += width
-            met = (far + swap(across, 1).astype(F32)).astype(BF16)
-            own = own + swap(near, 1).astype(F32)
-            back = swap(met, 2)
-            h, met = lax.optimization_barrier((h, met))
-            parts.append((own, back))
-        y = jnp.concatenate([(own + back.astype(F32)).astype(BF16) for own, back in parts], axis=1)
+        y = finish(h, w_down, c)
         return y[None, None]
 
     data, weights = P("dp", "ep"), P("ep")

time: 606 us -> 481 us (0.79)
  waiting for transfers between devices: 153 us -> 94.6 us
  Pallas kernels: 399 us -> 357 us
  other arithmetic: 25.1 us -> 5.83 us
    ppermute x21 -> x6, waiting for transfers between devices: 153 us -> 94.6 us  [swap(): return lax.ppermute(v, 'ep', [(i, i ^ bit) for i in range(members)])]
    pallas_call x5 -> x1, Pallas kernels: 178 us -> 135 us  [finish(): pl.pallas_call(kernel, out_shape=jax.ShapeDtypeStruct((tokens, d), BF16),...]
    convert_element_type x5 -> x0, other arithmetic: 11.3 us -> none  [whole(): met = (far + swap(across, 1).astype(F32)).astype(BF16)]
    unnamed x4 -> x0, other arithmetic: 7.55 us -> none
  transfers between devices with their start and end apart: 21 -> 6, of which waited for: 9 -> 2; matrix products, arithmetic and copies ran while one was open for 5% -> 3% of each run, Pallas kernels for 18% -> 11%
where the time goes in v2:
time: 481 us; the launch traced here: 476 us
  Pallas kernels  357 us (74%)
  waiting for transfers between devices  94.6 us (20%)
  local copies, waits for them, and re-layouts  13 us (3%)
  other arithmetic  5.83 us (1%)
  starting transfers between devices  5.58 us (1%)
    pallas_call x1, Pallas kernels, up(): pl.pallas_call(kernel, out_shape=jax.ShapeDtypeStruct((experts, rows, ff)...  156 us
    pallas_call x1, Pallas kernels, finish(): pl.pallas_call(kernel, out_shape=jax.ShapeDtypeStruct((tokens, d), BF16),...  135 us
    ppermute x6, waiting for transfers between devices, swap(): return lax.ppermute(v, 'ep', [(i, i ^ bit) for i in range(members)])  94.6 us
    pallas_call x4, Pallas kernels, dispatch(): pl.pallas_call(kernel, out_shape=jax.ShapeDtypeStruct((rows, d), BF16), g...  48 us
    pallas_call x1, Pallas kernels, combine_matrix(): pl.pallas_call(kernel, out_shape=jax.ShapeDtypeStruct((sources, tokens, r...  17.9 us
  transfers between devices with their start and end apart: 6, of which 2 were waited for; matrix products, arithmetic and copies ran while one was open for 3% of the time, Pallas kernels for 11%

profile of v2, /device:TPU:0, one launch (start us, length us, event | category | flops | bytes accessed | tf_op | source)
XLA Modules:
  0.0 476.0 jit_solution(13464508759689056786)
XLA Ops:
  0.0 3.3 collective-permute-start.4
  3.3 0.7 convert_bitcast_fusion
  4.0 0.7 convert_bitcast_fusion.1
  4.8 89.4 %collective-permute-done.4.x_ref = bf16[512,4096]{1,0:T(8,128)(2,1)} collective-permute-done((bf16[512,4096]{1,0:T(8,128)(2,1)}, bf16[512,4096]{1,0:T(8,128)(2,1)}, u32[]{:S(2)}, u32[]{:S(2)}) %collective-permute-start.4) | collective-permute-done | bytes 4194336 | tf_op jit(solution)/shard_map/ppermute | solution.py:309
  94.7 1.7 collective-permute-start.1
  96.5 5.2 %collective-permute-done = f32[24,512]{1,0:T(8,128)S(1)} collective-permute-done((f32[24,512]{1,0:T(8,128)S(1)}, f32[24,512]{1,0:T(8,128)S(1)}, u32[]{:S(2)}, u32[]{:S(2)}) %collective-permute-start) | collective-permute-done | bytes 49184 | tf_op jit(solution)/shard_map/ppermute | solution.py:309
  102.4 1.3 subtract_select_fusion
  103.7 1.5 copy.30
  105.6 1.2 select_reduce_fusion.1.count_ref
  107.4 1.4 select_bitcast_fusion
  108.9 0.7 copy.36.place_ref
  109.6 0.7 copy.34.place_ref
  110.3 0.7 copy.35.place_ref
  111.0 0.7 copy.33.place_ref
  111.8 0.7 copy.37.expert_at_ref
  112.5 1.3 copy.38
  113.8 17.9 %combine_matrix.1.c_hbm = bf16[4,512,1280]{2,1,0:T(8,128)(2,1)} custom-call(s32[4,512,8]{2,1,0:T(8,128)} %get-tuple-element.5.place_ref, f32[4,512,8]{2,1,0:T(8,128)} %bitcast.52), custom_call_target="tpu_custom_call" | custom-call | flops 62914560 | bytes 5242880 | tf_op jit(solution)/shard_map/combine_matrix/pallas_call | solution.py:75
  132.3 12.0 %dispatch.4.refs_0_ = bf16[1280,4096]{1,0:T(8,128)(2,1)} custom-call(s32[1]{0:T(128)} %bitcast.11.used_ref, s32[8,512]{1,0:T(8,128)} %copy.33.place_ref, bf16[512,4096]{1,0:T(8,128)(2,1)} %bitcast.60), custom_call_target="tpu_custom_call" | custom-call | flops 5368709120 | bytes 14680064 | tf_op jit(solution)/shard_map/dispatch/pallas_call | solution.py:44
  144.4 12.0 %dispatch.6.refs_2_ = bf16[1280,4096]{1,0:T(8,128)(2,1)} custom-call(s32[1]{0:T(128)} %bitcast.16.used_ref, s32[8,512]{1,0:T(8,128)} %copy.35.place_ref, bf16[512,4096]{1,0:T(8,128)(2,1)} %collective-permute-done.4.x_ref), custom_call_target="tpu_custom_call" | custom-call | flops 5368709120 | bytes 14680064 | tf_op jit(solution)/shard_map/dispatch/pallas_call | solution.py:44
  156.3 12.0 %dispatch.5.refs_1_ = bf16[1280,4096]{1,0:T(8,128)(2,1)} custom-call(s32[1]{0:T(128)} %bitcast.14.used_ref, s32[8,512]{1,0:T(8,128)} %copy.34.place_ref, bf16[512,4096]{1,0:T(8,128)(2,1)} %collective-permute-done.3.x_ref), custom_call_target="tpu_custom_call" | custom-call | flops 5368709120 | bytes 14680064 | tf_op jit(solution)/shard_map/dispatch/pallas_call | solution.py:44
  168.3 12.0 %dispatch.7.refs_3_ = bf16[1280,4096]{1,0:T(8,128)(2,1)} custom-call(s32[1]{0:T(128)} %bitcast.18.used_ref, s32[8,512]{1,0:T(8,128)} %copy.36.place_ref, bf16[512,4096]{1,0:T(8,128)(2,1)} %collective-permute-done.5.x_ref), custom_call_target="tpu_custom_call" | custom-call | flops 5368709120 | bytes 14680064 | tf_op jit(solution)/shard_map/dispatch/pallas_call | solution.py:44
  180.3 155.7 %up.1.h_hbm = bf16[16,320,1536]{2,1,0:T(8,128)(2,1)} custom-call(s32[4,16]{1,0:T(4,128)} %copy-done.1, s32[4,17]{1,0:T(4,128)} %copy-done, s32[16,5]{1,0:T(8,128)} %copy.37.expert_at_ref, bf16[1280,4096]{1,0:T(8,128)(2,1)} %dispatch.4.refs_0_, bf16[1280,4096]{1,0:T(8,128)(2,1)} %dispatch.5.refs_1_, bf16[1280,4096]{1,0:T(8,128)(2,1)} %dispatch.6.refs_2_, ...), custom_call_target="tpu_custom_call" | custom-call | flops 128849018880 | bytes 402653184 | tf_op jit(solution)/shard_map/up/pallas_call | solution.py:138
  336.0 135.2 %finish.1 = bf16[512,4096]{1,0:T(8,128)(2,1)} custom-call(bf16[16,320,1536]{2,1,0:T(8,128)(2,1)} %up.1.h_hbm, bf16[16,1536,4096]{2,1,0:T(8,128)(2,1)} %w_ref.1, bf16[4,512,1280]{2,1,0:T(8,128)(2,1)} %combine_matrix.1.c_hbm), custom_call_target="tpu_custom_call" | custom-call | flops 64424509440 | bytes 201326592 | tf_op jit(solution)/shard_map/finish/pallas_call | solution.py:276
  471.3 4.7 copy.40
  (28 shorter events, 3.0 us)
Async XLA Ops:
  0.0 94.2 %collective-permute-start.4 = (bf16[512,4096]{1,0:T(8,128)(2,1)}, bf16[512,4096]{1,0:T(8,128)(2,1)}, u32[]{:S(2)}, u32[]{:S(2)}) collective-permute-start(bf16[512,4096]{1,0:T(8,128)(2,1)} %bitcast.58), channel_id=1, source_target_pairs={{0,2},{1,3},{2,0},{3,1},{4,6},{5,7},{6,4},{7,5}} | collective-permute-start | bytes 12582920 | tf_op jit(solution)/shard_map/ppermute | solution.py:309
  3.3 153.0 %collective-permute-start.3 = (bf16[512,4096]{1,0:T(8,128)(2,1)}, bf16[512,4096]{1,0:T(8,128)(2,1)}, u32[]{:S(2)}, u32[]{:S(2)}) collective-permute-start(bf16[512,4096]{1,0:T(8,128)(2,1)} %bitcast.59), channel_id=1, source_target_pairs={{0,1},{1,0},{2,3},{3,2},{4,5},{5,4},{6,7},{7,6}} | collective-permute-start | bytes 12582920 | tf_op jit(solution)/shard_map/ppermute | solution.py:309
  94.2 74.1 %collective-permute-start.5 = (bf16[512,4096]{1,0:T(8,128)(2,1)}, bf16[512,4096]{1,0:T(8,128)(2,1)}, u32[]{:S(2)}, u32[]{:S(2)}) collective-permute-start(bf16[512,4096]{1,0:T(8,128)(2,1)} %collective-permute-done.4.x_ref), channel_id=1, source_target_pairs={{0,1},{1,0},{2,3},{3,2},{4,5},{5,4},{6,7},{7,6}} | collective-permute-start | bytes 12582920 | tf_op jit(solution)/shard_map/ppermute | solution.py:309
  94.2 7.5 %collective-permute-start = (f32[24,512]{1,0:T(8,128)S(1)}, f32[24,512]{1,0:T(8,128)S(1)}, u32[]{:S(2)}, u32[]{:S(2)}) collective-permute-start(f32[24,512]{1,0:T(8,128)S(1)} %get-tuple-element.17), channel_id=1, source_target_pairs={{0,1},{1,0},{2,3},{3,2},{4,5},{5,4},{6,7},{7,6}} | collective-permute-start | bytes 147464 | tf_op jit(solution)/shard_map/ppermute | solution.py:309
  94.7 7.0 %collective-permute-start.1 = (f32[24,512]{1,0:T(8,128)S(1)}, f32[24,512]{1,0:T(8,128)S(1)}, u32[]{:S(2)}, u32[]{:S(2)}) collective-permute-start(f32[24,512]{1,0:T(8,128)S(1)} %get-tuple-element.17), channel_id=1, source_target_pairs={{0,2},{1,3},{2,0},{3,1},{4,6},{5,7},{6,4},{7,5}} | collective-permute-start | bytes 147464 | tf_op jit(solution)/shard_map/ppermute | solution.py:309
  96.5 5.2 %collective-permute-start.2 = (f32[24,512]{1,0:T(8,128)S(1)}, f32[24,512]{1,0:T(8,128)S(1)}, u32[]{:S(2)}, u32[]{:S(2)}) collective-permute-start(f32[24,512]{1,0:T(8,128)S(1)} %get-tuple-element.17), channel_id=1, source_target_pairs={{0,3},{1,2},{2,1},{3,0},{4,7},{5,6},{6,5},{7,4}} | collective-permute-start | bytes 147464 | tf_op jit(solution)/shard_map/ppermute | solution.py:309
  106.8 37.5 %copy-start.1 = (s32[4,16]{1,0:T(4,128)}, s32[4,16]{1,0:T(4,128)S(1)}, u32[]{:S(2)}) copy-start(s32[4,16]{1,0:T(4,128)S(1)} %select_reduce_fusion.1.count_ref) | copy-start | bytes 772
  106.9 37.4 %copy-start = (s32[4,17]{1,0:T(4,128)}, s32[4,17]{1,0:T(4,128)S(1)}, u32[]{:S(2)}) copy-start(s32[4,17]{1,0:T(4,128)S(1)} %select_reduce_fusion.2.source_at_ref) | copy-start | bytes 820

commit v3 on v2

v3 whole, which is shorter than its diff:
```python
import jax
import jax.numpy as jnp
from jax import lax
from jax.experimental import pallas as pl
from jax.experimental.pallas import tpu as pltpu
from jax.sharding import PartitionSpec as P

F32, BF16, I32 = jnp.float32, jnp.bfloat16, jnp.int32
VMEM_LIMIT = 64 * 1024 * 1024 - 64 * 1024 * 2
GROUP = 16
ANY = pl.BlockSpec(memory_space=pl.ANY)


def params(*semantics):
    return pltpu.CompilerParams(dimension_semantics=semantics, vmem_limit_bytes=VMEM_LIMIT)


def places(routes, experts, slots):
    sources = len(routes)
    top, tokens = routes[0].shape[0] // 3, routes[0].shape[1]

    def kernel(*refs):
        route_refs, (place_ref, pair_ref, count_ref, source_at_ref, expert_at_ref) = refs[:sources], refs[sources:]
        base = lax.axis_index("ep") * experts
        for a in range(sources):
            mine = route_refs[a][:top, :].astype(I32) - base
            slot = route_refs[a][top:2 * top, :].astype(I32)
            kept = (mine >= 0) & (mine < experts) & (slot < slots)
            mine = jnp.where(kept, mine, -1)
            gate = route_refs[a][2 * top:, :]
            here, place = jnp.int32(0), jnp.full((top, tokens), -1, I32)
            for e in range(experts):
                its = mine == e
                used = jnp.max(jnp.where(its, slot + 1, 0))
                count_ref[a, e] = used
                source_at_ref[a, e] = here
                place = jnp.where(its, slot + here, place)
                pair_ref[a, e:e + 1, :] = (jnp.max(jnp.where(its, slot + 1, 0), axis=0, keepdims=True) - 1).astype(F32)
                pair_ref[a, experts + e:experts + e + 1, :] = jnp.sum(jnp.where(its, gate, 0.0), axis=0, keepdims=True)
                here = here + (used + GROUP - 1) // GROUP * GROUP
            source_at_ref[a, experts] = here
            place_ref[a] = place
        for e in range(experts):
            here = jnp.int32(0)
            for a in range(sources):
                expert_at_ref[e, a] = here
                here = here + (count_ref[a, e] + GROUP - 1) // GROUP * GROUP
            expert_at_ref[e, sources] = here

    smem = pl.BlockSpec(memory_space=pltpu.SMEM)
    vmem = pl.BlockSpec(memory_space=pltpu.VMEM)
    return pl.pallas_call(
        kernel,
        out_shape=[
            jax.ShapeDtypeStruct((sources, top, tokens), I32),
            jax.ShapeDtypeStruct((sources, 2 * experts, tokens), F32),
            jax.ShapeDtypeStruct((sources, experts), I32),
            jax.ShapeDtypeStruct((sources, experts + 1), I32),
            jax.ShapeDtypeStruct((experts, sources + 1), I32),
        ],
        in_specs=[vmem] * sources,
        out_specs=[vmem, vmem, smem, smem, smem],
        cost_estimate=pl.CostEstimate(flops=1000000, bytes_accessed=400000, transcendentals=0),
        name="places",
    )(*routes)


def dispatch(rows_used, place, xs, rows):
    sources, top, tokens = place.shape
    width = xs[0].shape[1]
    block = 256
    tile = 1024

    def kernel(used_ref, place_ref, *refs):
        x_refs, z_ref = refs[:sources], refs[sources]
        i = pl.program_id(1)
        for a in range(sources):
            @pl.when((pl.program_id(0) == a) & (i * block < used_ref[a]))
            def _(a=a):
                row = lax.broadcasted_iota(I32, (block, tokens), 0) + i * block
                hit = row == place_ref[0, 0:1, :]
                for k in range(1, top):
                    hit = hit | (row == place_ref[0, k:k + 1, :])
                hot = jnp.where(hit, 1.0, 0.0).astype(BF16)
                for j in range(0, width, tile):
                    k = min(j + tile, width)
                    z_ref[0, :, j:k] = jnp.dot(hot, x_refs[a][:, j:k], preferred_element_type=F32).astype(BF16)

    return pl.pallas_call(
        kernel,
        out_shape=jax.ShapeDtypeStruct((sources, rows, width), BF16),
        grid_spec=pltpu.PrefetchScalarGridSpec(
            num_scalar_prefetch=1,
            grid=(sources, rows // block),
            in_specs=[pl.BlockSpec((1, top, tokens), lambda a, i, *_: (a, 0, 0))]
            + [pl.BlockSpec((tokens, width), lambda a, i, *_: (0, 0))] * sources,
            out_specs=pl.BlockSpec(
                (1, block, width),
                lambda a, i, used: (a, jnp.minimum(i, jnp.maximum(used[a] + block - 1, block) // block - 1), 0)),
        ),
        compiler_params=params("arbitrary", "arbitrary"),
        cost_estimate=pl.CostEstimate(
            flops=2 * sources * rows * tokens * width, bytes_accessed=4 * sources * rows * width, transcendentals=0),
        name="dispatch",
    )(rows_used, place, *xs)


def combine_matrix(pair, slots):
    sources, tokens, experts = pair.shape[0], pair.shape[1], pair.shape[2] // 2
    columns = experts * slots

    def kernel(pair_ref, c_ref):
        column = lax.broadcasted_iota(I32, (experts, columns), 1)
        own = lax.broadcasted_iota(I32, (experts, columns), 0)
        low = own * slots
        spread = jnp.where((column >= low) & (column < low + slots), 1.0, 0.0).astype(BF16)
        local = jnp.sum(jnp.where((column >= low) & (column < low + slots), column - low, 0), axis=0, keepdims=True).astype(F32)
        slot = jnp.dot(pair_ref[0, :, :experts].astype(BF16), spread, preferred_element_type=F32)
        gate = jnp.dot(pair_ref[0, :, experts:].astype(BF16), spread, preferred_element_type=F32)
        c_ref[0] = jnp.where(slot == local, gate, 0.0).astype(BF16)

    block = 256
    return pl.pallas_call(
        kernel,
        out_shape=jax.ShapeDtypeStruct((sources, tokens, columns), BF16),
        grid=(sources, tokens // block),
        in_specs=[pl.BlockSpec((1, block, 2 * experts), lambda a, i: (a, i, 0))],
        out_specs=pl.BlockSpec((1, block, columns), lambda a, i: (a, i, 0)),
        compiler_params=params("arbitrary", "arbitrary"),
        cost_estimate=pl.CostEstimate(flops=100000000, bytes_accessed=sources * tokens * columns * 2, transcendentals=0),
        name="combine_matrix",
    )(pair)


def up(first, depth, count, source_at, expert_at, z0, z2, z3, w_gate, w_up, slots, partial=None):
    experts, _, ff = w_gate.shape
    sources = count.shape[0]
    rows = sources * slots
    tile = 768 if depth <= 2048 else 512
    steps = ff // tile
    total = experts * steps
    unit = 64
    sizes = list(range(unit, rows + 1, unit))
    last = first > 0
    ahead, z_ahead, part_slots = 3, 2, 3

    def kernel(count_ref, source_at_ref, expert_at_ref, z0_ref, z2_ref, z3_ref, wg_hbm, wu_hbm, *refs):
        if last:
            partial_ref, h_ref, z_ref, part_ref, wg_ref, wu_ref, z_sem, part_sem, wg_sem, wu_sem, hs_ref = refs
        else:
            partial_ref, z_ref, part_ref, wg_ref, wu_ref, z_sem, part_sem, wg_sem, wu_sem = refs
        t = pl.program_id(0)
        e, f = t // steps, lax.rem(t, steps)
        now = lax.rem(t, part_slots)

        def start(c):
            c.start()

        def wait(c):
            c.wait()

        def weights(t, act):
            e, f, slot = t // steps, lax.rem(t, steps), lax.rem(t, ahead + 1)
            at = (e, pl.ds(first, depth), pl.ds(pl.multiple_of(f * tile, tile), tile))
            act(pltpu.make_async_copy(wg_hbm.at[at], wg_ref.at[slot], wg_sem.at[slot]))
            act(pltpu.make_async_copy(wu_hbm.at[at], wu_ref.at[slot], wu_sem.at[slot]))

        def inputs(e, act):
            slot = lax.rem(e, z_ahead + 1)
            for a in range(sources):
                source = (z0_ref.at[0], z0_ref.at[1], z2_ref.at[0], z3_ref.at[0])[a]
                columns = pl.ds(first if a < 2 else 0, depth)
                for g in range(slots // GROUP):
                    @pl.when(g * GROUP < count_ref[a, e])
                    def _(a=a, g=g, source=source, columns=columns):
                        act(pltpu.make_async_copy(
                            source.at[pl.ds(pl.multiple_of(source_at_ref[a, e] + g * GROUP, GROUP), GROUP), columns],
                            z_ref.at[slot, pl.ds(pl.multiple_of(expert_at_ref[e, a] + g * GROUP, GROUP), GROUP), :],
                            z_sem.at[slot, a, g]))

        def by_size(e, act):
            used = expert_at_ref[e, sources]
            for size in sizes:
                @pl.when((used > size - unit) & (used <= size))
                def _(size=size):
                    act(size)

        def sums(t, act):
            e, f, slot = t // steps, lax.rem(t, steps), lax.rem(t, part_slots)

            def one(size):
                here = part_ref.at[slot, :, pl.ds(0, size), :]
                there = partial_ref.at[e, :, pl.ds(0, size), pl.ds(pl.multiple_of(f * tile, tile), tile)]
                act(pltpu.make_async_copy(there, here, part_sem.at[slot]) if last
                    else pltpu.make_async_copy(here, there, part_sem.at[slot]))

            by_size(e, one)

        used = expert_at_ref[e, sources]

        @pl.when(t == 0)
        def _():
            for n in range(z_ahead):
                inputs(n, start)
            if last:
                for n in range(part_slots - 1):
                    sums(n, start)
            for n in range(ahead):
                weights(n, start)

        @pl.when(f == 0)
        def _():
            inputs(e, wait)

            @pl.when(e + z_ahead < experts)
            def _():
                inputs(e + z_ahead, start)

            z_ref[lax.rem(e, z_ahead + 1), pl.ds(pl.multiple_of(used, GROUP), unit), :] = jnp.zeros((unit, depth), BF16)

        if last:
            @pl.when(t + part_slots - 1 < total)
            def _():
                sums(t + part_slots - 1, start)

            sums(t, wait)
        else:
            @pl.when(t >= part_slots)
            def _():
                sums(t - part_slots, wait)

        @pl.when(t + ahead < total)
        def _():
            weights(t + ahead, start)

        weights(t, wait)

        def product(size):
            slot = lax.rem(t, ahead + 1)
            z = z_ref[lax.rem(e, z_ahead + 1), :size, :]
            a = jnp.dot(z, wg_ref[slot], preferred_element_type=F32)
            b = jnp.dot(z, wu_ref[slot], preferred_element_type=F32)
            if last:
                a, b = a + part_ref[now, 0, :size, :], b + part_ref[now, 1, :size, :]
                hs_ref[:size, :] = (jax.nn.silu(a) * b).astype(BF16)
            else:
                part_ref[now, 0, :size, :] = a
                part_ref[now, 1, :size, :] = b

        by_size(e, product)

        if last:
            hs_ref[pl.ds(pl.multiple_of(used, GROUP), slots), :] = jnp.zeros((slots, tile), BF16)
            for a in range(sources):
                h_ref[0, a * slots:(a + 1) * slots, :] = hs_ref[pl.ds(pl.multiple_of(expert_at_ref[e, a], GROUP), slots), :]
        else:
            sums(t, start)

            @pl.when(t == total - 1)
            def _():
                for n in range(total - part_slots, total):
                    sums(n, wait)

    dma = pltpu.SemaphoreType.DMA
    scratch = [
        pltpu.VMEM((z_ahead + 1, rows + unit, depth), BF16),
        pltpu.VMEM((part_slots, 2, rows, tile), F32),
        pltpu.VMEM((ahead + 1, depth, tile), BF16),
        pltpu.VMEM((ahead + 1, depth, tile), BF16),
        dma((z_ahead + 1, sources, slots // GROUP)),
        dma((part_slots,)),
        dma((ahead + 1,)),
        dma((ahead + 1,)),
    ]
    if last:
        out_shape = jax.ShapeDtypeStruct((experts, rows, ff), BF16)
        out_spec = pl.BlockSpec((1, rows, tile), lambda t, *_: (t // steps, 0, lax.rem(t, steps)))
        scratch.append(pltpu.VMEM((rows + slots, tile), BF16))
    else:
        out_shape, out_spec = jax.ShapeDtypeStruct((experts, 2, rows, ff), F32), ANY
    more = [partial] if last else []
    return pl.pallas_call(
        kernel,
        out_shape=out_shape,
        grid_spec=pltpu.PrefetchScalarGridSpec(
            num_scalar_prefetch=3,
            grid=(total,),
            in_specs=[ANY] * (5 + len(more)),
            out_specs=out_spec,
            scratch_shapes=scratch,
        ),
        compiler_params=params("arbitrary"),
        cost_estimate=pl.CostEstimate(
            flops=4 * experts * rows * depth * ff, bytes_accessed=4 * experts * depth * ff, transcendentals=0),
        name="up",
    )(count, source_at, expert_at, z0, z2, z3, w_gate, w_up, *more)


def finish(h, w_down, c):
    experts, rows, ff = h.shape
    sources, tokens, columns = c.shape
    d = w_down.shape[2]
    slots = rows // sources
    width, batch, lag = 512, 4, 2
    chunks, groups = d // width, experts // batch
    block = (tokens, width)

    def kernel(h_hbm, w_ref, c_hbm, y_hbm, h_ref, c_ref, out_ref, got3, got1, met, send3, send1, send2, far, own, y_ref,
               h_sem, c_sem, y_sem, send3_sem, send1_sem, send2_sem, got3_sem, got1_sem, met_sem):
        chunk, group = pl.program_id(0), pl.program_id(1)
        me = lax.axis_index("ep")
        beside = me + 1 - 2 * lax.rem(me, 2)
        across = lax.rem(me + 2, 4)
        half = lax.rem(chunk, 2)

        def load_h(g):
            at = pl.ds(pl.multiple_of(g * batch, batch), batch)
            return pltpu.make_async_copy(h_hbm.at[at], h_ref.at[at], h_sem.at[g])

        load_c = pltpu.make_async_copy(c_hbm, c_ref, c_sem)

        def remote(source, target, slot, sent, got, number, to):
            return pltpu.make_async_remote_copy(
                src_ref=source.at[slot], dst_ref=target.at[number], send_sem=sent.at[slot], recv_sem=got.at[number],
                device_id={"ep": to}, device_id_type=pl.DeviceIdType.MESH)

        def to_beside3(n):
            return remote(send3, got3, lax.rem(n, 2), send3_sem, got3_sem, n, beside)

        def to_beside1(n):
            return remote(send1, got1, lax.rem(n, 2), send1_sem, got1_sem, n, beside)

        def to_across(n):
            return remote(send2, met, lax.rem(n, 2), send2_sem, met_sem, n, across)

        def write(n):
            return pltpu.make_async_copy(
                y_ref.at[lax.rem(n, 2)], y_hbm.at[:, pl.ds(pl.multiple_of(n * width, width), width)], y_sem.at[lax.rem(n, 2)])

        @pl.when((chunk == 0) & (group == 0))
        def _():
            for g in range(groups):
                load_h(g).start()
            load_c.start()
            barrier = pltpu.get_barrier_semaphore()
            for to in (beside, across):
                pl.semaphore_signal(barrier, inc=1, device_id={"ep": to}, device_id_type=pl.DeviceIdType.MESH)
            pl.semaphore_wait(barrier, 2)

        @pl.when(chunk == 0)
        def _():
            load_h(group).wait()

        for i in range(batch):
            e = group * batch + i
            o = jnp.dot(h_ref[e], w_ref[i], preferred_element_type=F32).astype(BF16)
            for a in range(sources):
                out_ref[a, pl.ds(pl.multiple_of(e * slots, GROUP), slots), :] = o[a * slots:(a + 1) * slots]

        @pl.when(group == groups - 1)
        def _():
            @pl.when(chunk == 0)
            def _():
                load_c.wait()

            @pl.when(chunk >= 2)
            def _():
                to_beside3(chunk - 2).wait_send()
                to_beside1(chunk - 2).wait_send()
                to_across(chunk - 2).wait_send()

            def share(a):
                return jnp.dot(c_ref[a], out_ref[a], preferred_element_type=F32)

            send3[half] = share(3).astype(BF16)
            send1[half] = share(1).astype(BF16)
            to_beside3(chunk).start()
            far[...] = share(2)
            to_beside1(chunk).start()
            own[lax.rem(chunk, lag + 1)] = share(0)
            to_beside3(chunk).wait_recv()
            send2[half] = (far[...] + got3[chunk].astype(F32)).astype(BF16)

            def close(n):
                to_beside1(n).wait_recv()
                to_across(n).wait_recv()

                @pl.when(n >= 2)
                def _():
                    write(n - 2).wait()

                y_ref[lax.rem(n, 2)] = (
                    own[lax.rem(n, lag + 1)] + got1[n].astype(F32) + met[n].astype(F32)).astype(BF16)
                write(n).start()

            to_across(chunk).start()

            @pl.when(chunk >= lag)
            def _():
                close(chunk - lag)

            @pl.when(chunk == chunks - 1)
            def _():
                for n in range(chunks - lag, chunks):
                    close(n)
                for n in range(chunks - 2, chunks):
                    to_beside3(n).wait_send()
                    to_beside1(n).wait_send()
                    to_across(n).wait_send()
                    write(n).wait()

    dma = pltpu.SemaphoreType.DMA
    return pl.pallas_call(
        kernel,
        out_shape=jax.ShapeDtypeStruct((tokens, d), BF16),
        grid=(chunks, groups),
        in_specs=[ANY, pl.BlockSpec((batch, ff, width), lambda n, g: (g, 0, n)), ANY],
        out_specs=ANY,
        scratch_shapes=[
            pltpu.VMEM((experts, rows, ff), BF16),
            pltpu.VMEM((sources, tokens, columns), BF16),
            pltpu.VMEM((sources, columns, width), BF16),
            pltpu.VMEM((chunks, *block), BF16),
            pltpu.VMEM((chunks, *block), BF16),
            pltpu.VMEM((chunks, *block), BF16),
            pltpu.VMEM((2, *block), BF16),
            pltpu.VMEM((2, *block), BF16),
            pltpu.VMEM((2, *block), BF16),
            pltpu.VMEM(block, F32),
            pltpu.VMEM((lag + 1, *block), F32),
            pltpu.VMEM((2, *block), BF16),
            dma((groups,)), dma, dma((2,)), dma((2,)), dma((2,)), dma((2,)), dma((chunks,)), dma((chunks,)), dma((chunks,)),
        ],
        compiler_params=pltpu.CompilerParams(
            dimension_semantics=("arbitrary", "arbitrary"), vmem_limit_bytes=VMEM_LIMIT, collective_id=0, has_side_effects=True),
        cost_estimate=pl.CostEstimate(
            flops=2 * experts * rows * ff * d, bytes_accessed=2 * experts * ff * d, transcendentals=0),
        name="finish",
    )(h, w_down, c)


def solution(mesh):
    members = mesh.shape["ep"]

    def swap(v, bit):
        return lax.ppermute(v, "ep", [(i, i ^ bit) for i in range(members)])

    def whole(x, expert, slot, gate, w_gate, w_up, w_down):
        tokens, top = expert.shape[2:]
        experts = w_gate.shape[0]
        slots = 5 * tokens * top // (4 * experts * members)
        rows = experts * slots
        x, expert, slot, gate = x[0, 0], expert[0, 0], slot[0, 0], gate[0, 0]

        routing = jnp.concatenate([
            expert.T.astype(F32), jnp.minimum(slot, slots).T.astype(F32), gate.T.astype(BF16).astype(F32)])
        near = swap(routing, 1)
        far = swap(routing, 2)
        across = swap(routing, 3)
        x1 = swap(x, 1)
        middle = 3 * x.shape[1] // 8
        x2a = swap(x[:, :middle], 2)
        x3a = swap(x2a, 1)
        place, pair, count, source_at, expert_at = places((routing, near, far, across), experts, slots)
        used = source_at[:, experts:]
        counts, rest = [used[:2, 0], used[2], used[3]], x[:, middle:]
        put = [place[:2], place[2:3], place[3:]]
        counts, put, pair, xb = lax.optimization_barrier((counts, put, pair.swapaxes(1, 2), rest))
        x2b = swap(xb, 2)
        x3b = swap(x2b, 1)
        z0 = dispatch(counts[0], put[0], (x, x1), rows)
        c = combine_matrix(pair, slots)
        z2 = dispatch(counts[1], put[1], (x2a,), rows)
        z3 = dispatch(counts[2], put[2], (x3a,), rows)
        partial = up(0, middle, count, source_at, expert_at, z0, z2, z3, w_gate, w_up, slots)
        z2 = dispatch(counts[1], put[1], (x2b,), rows)
        z3 = dispatch(counts[2], put[2], (x3b,), rows)
        h = up(middle, x.shape[1] - middle, count, source_at, expert_at, z0, z2, z3, w_gate, w_up, slots, partial=partial)
        y = finish(h, w_down, c)
        return y[None, None]

    data, weights = P("dp", "ep"), P("ep")
    return jax.shard_map(
        whole, mesh=mesh, in_specs=(data,) * 4 + (weights,) * 3, out_specs=data, check_vma=False)
```

time: 481 us -> 439 us (0.913)
  waiting for transfers between devices: 94.6 us -> 61.9 us
  Pallas kernels: 357 us -> 344 us
  local copies, waits for them, and re-layouts: 13 us -> 18.6 us
    ppermute x6 -> x8, waiting for transfers between devices: 94.6 us -> 61.9 us  [swap(): return lax.ppermute(v, 'ep', [(i, i ^ bit) for i in range(members)])]
    slice x3 -> x6, local copies, waits for them, and re-layouts: 2.26 us -> 10.4 us  [the longest x3 6.2 us: whole(): counts, rest = ([used[:2, 0], used[2], used[3]], x[:, middle:])]
    pallas_call x1, Pallas kernels: 135 us -> 127 us  [finish(): pl.pallas_call(kernel, out_shape=jax.ShapeDtypeStruct((tokens, d), BF16),...]
    pallas_call x6 -> x9, Pallas kernels: 222 us -> 217 us  [the longest x2 164 us: up(): pl.pallas_call(kernel, out_shape=out_shape, grid_spec=pltpu.PrefetchScala...]
  transfers between devices with their start and end apart: 6 -> 8, of which waited for: 2 -> 2; matrix products, arithmetic and copies ran while one was open for 3% -> 3% of each run, Pallas kernels for 11% -> 25%
where the time goes in v3:
time: 439 us; the launch traced here: 432 us
  Pallas kernels  344 us (78%)
  waiting for transfers between devices  61.9 us (14%)
  local copies, waits for them, and re-layouts  18.6 us (4%)
  starting transfers between devices  5.89 us (1%)
    pallas_call x2, Pallas kernels, up(): pl.pallas_call(kernel, out_shape=out_shape, grid_spec=pltpu.PrefetchScala...  164 us
    pallas_call x1, Pallas kernels, finish(): pl.pallas_call(kernel, out_shape=jax.ShapeDtypeStruct((tokens, d), BF16),...  127 us
    ppermute x8, waiting for transfers between devices, swap(): return lax.ppermute(v, 'ep', [(i, i ^ bit) for i in range(members)])  61.9 us
    pallas_call x5, Pallas kernels, dispatch(): pl.pallas_call(kernel, out_shape=jax.ShapeDtypeStruct((sources, rows, wid...  42.1 us
  transfers between devices with their start and end apart: 8, of which 2 were waited for; matrix products, arithmetic and copies ran while one was open for 3% of the time, Pallas kernels for 25%

profile of v3, /device:TPU:0, one launch (start us, length us, event | category | flops | bytes accessed | tf_op | source)
XLA Modules:
  0.0 431.8 jit_solution(7822970943929042084)
XLA Ops:
  0.0 0.8 collective-permute-start.3
  1.6 0.7 convert_bitcast_fusion.1
  2.3 3.0 collective-permute-start.1
  5.3 1.5 slice.37
  6.8 1.4 collective-permute-start.6
  8.2 3.4 slice.36
  12.9 3.1 places.1
  16.0 1.4 slice.31.place_ref
  17.3 2.3 copy.9
  19.6 1.4 slice_reduce_fusion.used_ref
  21.0 1.4 fusion.1
  22.4 1.4 fusion
  24.4 19.8 %collective-permute-done.6.refs_0_ = bf16[512,1536]{1,0:T(8,128)(2,1)} collective-permute-done((bf16[512,1536]{1,0:T(8,128)(2,1)S(1)}, bf16[512,1536]{1,0:T(8,128)(2,1)}, u32[]{:S(2)}, u32[]{:S(2)}) %collective-permute-start.6) | collective-permute-done | bytes 1572896 | tf_op jit(solution)/shard_map/ppermute | solution.py:446
  44.2 7.7 %combine_matrix.1.c_hbm = bf16[4,512,1280]{2,1,0:T(8,128)(2,1)} custom-call(f32[4,512,32]{2,1,0:T(8,128)} %bitcast.23), custom_call_target="tpu_custom_call" | custom-call | flops 100000000 | bytes 5242880 | tf_op jit(solution)/shard_map/combine_matrix/pallas_call | solution.py:123
  52.0 5.8 %dispatch.8.z2_ref = bf16[1,1280,1536]{2,1,0:T(8,128)(2,1)} custom-call(s32[1]{0:T(128)} %bitcast.6.used_ref, s32[1,8,512]{2,1,0:T(8,128)} %get-tuple-element.26.place_ref, bf16[512,1536]{1,0:T(8,128)(2,1)} %collective-permute-done.6.refs_0_), custom_call_target="tpu_custom_call" | custom-call | flops 2013265920 | bytes 7864320 | tf_op jit(solution)/shard_map/dispatch/pallas_call | solution.py:89
  57.8 42.0 %collective-permute-done.4.refs_0_ = bf16[512,2560]{1,0:T(8,128)(2,1)} collective-permute-done((bf16[512,2560]{1,0:T(8,128)(2,1)}, bf16[512,2560]{1,0:T(8,128)(2,1)}, u32[]{:S(2)}, u32[]{:S(2)}) %collective-permute-start.4) | collective-permute-done | bytes 2621472 | tf_op jit(solution)/shard_map/ppermute | solution.py:446
  99.8 7.2 %dispatch.6.z2_ref = bf16[1,1280,2560]{2,1,0:T(8,128)(2,1)} custom-call(s32[1]{0:T(128)} %bitcast.6.used_ref, s32[1,8,512]{2,1,0:T(8,128)} %get-tuple-element.26.place_ref, bf16[512,2560]{1,0:T(8,128)(2,1)} %collective-permute-done.4.refs_0_), custom_call_target="tpu_custom_call" | custom-call | flops 3355443200 | bytes 13107200 | tf_op jit(solution)/shard_map/dispatch/pallas_call | solution.py:89
  107.0 5.8 %dispatch.9.z3_ref = bf16[1,1280,1536]{2,1,0:T(8,128)(2,1)} custom-call(s32[1]{0:T(128)} %bitcast.7.used_ref, s32[1,8,512]{2,1,0:T(8,128)} %get-tuple-element.29.place_ref, bf16[512,1536]{1,0:T(8,128)(2,1)} %collective-permute-done.7.refs_0_), custom_call_target="tpu_custom_call" | custom-call | flops 2013265920 | bytes 7864320 | tf_op jit(solution)/shard_map/dispatch/pallas_call | solution.py:89
  112.8 16.3 %dispatch.5.z0_ref = bf16[2,1280,4096]{2,1,0:T(8,128)(2,1)} custom-call(s32[2]{0:T(128)} %slice_reduce_fusion.used_ref, s32[2,8,512]{2,1,0:T(8,128)} %slice.31.place_ref, bf16[512,4096]{1,0:T(8,128)(2,1)} %bitcast.21, bf16[512,4096]{1,0:T(8,128)(2,1)} %collective-permute-done.3.refs_1_), custom_call_target="tpu_custom_call" | custom-call | flops 10737418240 | bytes 41943040 | tf_op jit(solution)/shard_map/dispatch/pallas_call | solution.py:89
  129.1 64.0 %up.2.refs_0_ = f32[16,2,320,1536]{3,2,1,0:T(8,128)} custom-call(s32[4,16]{1,0:T(4,128)} %get-tuple-element.18.count_ref, s32[4,17]{1,0:T(4,128)} %get-tuple-element.19.source_at_ref, s32[16,5]{1,0:T(8,128)} %get-tuple-element.20.expert_at_ref, bf16[2,1280,4096]{2,1,0:T(8,128)(2,1)} %dispatch.5.z0_ref, bf16[1,1280,1536]{2,1,0:T(8,128)(2,1)} %dispatch.8.z2_ref, ...), custom_call_target="tpu_custom_call" | custom-call | flops 48318382080 | bytes 150994944 | tf_op jit(solution)/shard_map/up/pallas_call | solution.py:282
  193.1 7.1 %dispatch.7.z3_ref = bf16[1,1280,2560]{2,1,0:T(8,128)(2,1)} custom-call(s32[1]{0:T(128)} %bitcast.7.used_ref, s32[1,8,512]{2,1,0:T(8,128)} %get-tuple-element.29.place_ref, bf16[512,2560]{1,0:T(8,128)(2,1)} %collective-permute-done.5.refs_0_), custom_call_target="tpu_custom_call" | custom-call | flops 3355443200 | bytes 13107200 | tf_op jit(solution)/shard_map/dispatch/pallas_call | solution.py:89
  200.2 99.9 %up.3.h_hbm = bf16[16,320,1536]{2,1,0:T(8,128)(2,1)} custom-call(s32[4,16]{1,0:T(4,128)} %get-tuple-element.18.count_ref, s32[4,17]{1,0:T(4,128)} %get-tuple-element.19.source_at_ref, s32[16,5]{1,0:T(8,128)} %get-tuple-element.20.expert_at_ref, bf16[2,1280,4096]{2,1,0:T(8,128)(2,1)} %dispatch.5.z0_ref, bf16[1,1280,2560]{2,1,0:T(8,128)(2,1)} %dispatch.6.z2_ref, ...), custom_call_target="tpu_custom_call" | custom-call | flops 80530636800 | bytes 251658240 | tf_op jit(solution)/shard_map/up/pallas_call | solution.py:282
  300.0 127.0 %finish.1 = bf16[512,4096]{1,0:T(8,128)(2,1)} custom-call(bf16[16,320,1536]{2,1,0:T(8,128)(2,1)} %up.3.h_hbm, bf16[16,1536,4096]{2,1,0:T(8,128)(2,1)} %w_ref.1, bf16[4,512,1280]{2,1,0:T(8,128)(2,1)} %combine_matrix.1.c_hbm), custom_call_target="tpu_custom_call" | custom-call | flops 64424509440 | bytes 201326592 | tf_op jit(solution)/shard_map/finish/pallas_call | solution.py:413
  427.1 4.7 %copy.11 = bf16[1,1,512,4096]{3,2,1,0:T(8,128)(2,1)} copy(bf16[1,1,512,4096]{3,2,1,0:T(8,128)(2,1)} %bitcast.22) | data formatting | bytes 8388608
  (21 shorter events, 2.6 us)
Async XLA Ops:
  0.0 112.8 %collective-permute-start.3 = (bf16[512,4096]{1,0:T(8,128)(2,1)}, bf16[512,4096]{1,0:T(8,128)(2,1)}, u32[]{:S(2)}, u32[]{:S(2)}) collective-permute-start(bf16[512,4096]{1,0:T(8,128)(2,1)} %bitcast.18), channel_id=1, source_target_pairs={{0,1},{1,0},{2,3},{3,2},{4,5},{5,4},{6,7},{7,6}} | collective-permute-start | bytes 12582920 | tf_op jit(solution)/shard_map/ppermute | solution.py:446
  2.3 9.4 %copy-start = (f32[24,512]{1,0:T(8,128)}, f32[24,512]{1,0:T(8,128)S(1)}, u32[]{:S(2)}) copy-start(f32[24,512]{1,0:T(8,128)S(1)} %pad_maximum_fusion.refs_0_) | copy-start | bytes 147460
  2.3 9.3 %collective-permute-start = (f32[24,512]{1,0:T(8,128)S(1)}, f32[24,512]{1,0:T(8,128)S(1)}, u32[]{:S(2)}, u32[]{:S(2)}) collective-permute-start(f32[24,512]{1,0:T(8,128)S(1)} %pad_maximum_fusion.refs_0_), channel_id=1, source_target_pairs={{0,1},{1,0},{2,3},{3,2},{4,5},{5,4},{6,7},{7,6}} | collective-permute-start | bytes 147464 | tf_op jit(solution)/shard_map/ppermute | solution.py:446
  2.3 9.3 %collective-permute-start.1 = (f32[24,512]{1,0:T(8,128)S(1)}, f32[24,512]{1,0:T(8,128)S(1)}, u32[]{:S(2)}, u32[]{:S(2)}) collective-permute-start(f32[24,512]{1,0:T(8,128)S(1)} %pad_maximum_fusion.refs_0_), channel_id=1, source_target_pairs={{0,2},{1,3},{2,0},{3,1},{4,6},{5,7},{6,4},{7,5}} | collective-permute-start | bytes 147464 | tf_op jit(solution)/shard_map/ppermute | solution.py:446
  5.3 6.4 %collective-permute-start.2 = (f32[24,512]{1,0:T(8,128)S(1)}, f32[24,512]{1,0:T(8,128)S(1)}, u32[]{:S(2)}, u32[]{:S(2)}) collective-permute-start(f32[24,512]{1,0:T(8,128)S(1)} %pad_maximum_fusion.refs_0_), channel_id=1, source_target_pairs={{0,3},{1,2},{2,1},{3,0},{4,7},{5,6},{6,5},{7,4}} | collective-permute-start | bytes 147464 | tf_op jit(solution)/shard_map/ppermute | solution.py:446
  6.8 37.4 %collective-permute-start.6 = (bf16[512,1536]{1,0:T(8,128)(2,1)S(1)}, bf16[512,1536]{1,0:T(8,128)(2,1)}, u32[]{:S(2)}, u32[]{:S(2)}) collective-permute-start(bf16[512,1536]{1,0:T(8,128)(2,1)S(1)} %slice.37), channel_id=1, source_target_pairs={{0,2},{1,3},{2,0},{3,1},{4,6},{5,7},{6,4},{7,5}} | collective-permute-start | bytes 4718600 | tf_op jit(solution)/shard_map/ppermute | solution.py:446
  11.7 0.6 copy-start.1
  11.7 0.6 copy-start.2
  12.3 0.6 copy-start.3
  23.7 76.1 %collective-permute-start.4 = (bf16[512,2560]{1,0:T(8,128)(2,1)}, bf16[512,2560]{1,0:T(8,128)(2,1)}, u32[]{:S(2)}, u32[]{:S(2)}) collective-permute-start(bf16[512,2560]{1,0:T(8,128)(2,1)} %slice.36), channel_id=1, source_target_pairs={{0,2},{1,3},{2,0},{3,1},{4,6},{5,7},{6,4},{7,5}} | collective-permute-start | bytes 7864328 | tf_op jit(solution)/shard_map/ppermute | solution.py:446
  44.2 62.8 %collective-permute-start.7 = (bf16[512,1536]{1,0:T(8,128)(2,1)}, bf16[512,1536]{1,0:T(8,128)(2,1)}, u32[]{:S(2)}, u32[]{:S(2)}) collective-permute-start(bf16[512,1536]{1,0:T(8,128)(2,1)} %collective-permute-done.6.refs_0_), channel_id=1, source_target_pairs={{0,1},{1,0},{2,3},{3,2},{4,5},{5,4},{6,7},{7,6}} | collective-permute-start | bytes 4718600 | tf_op jit(solution)/shard_map/ppermute | solution.py:446
  99.8 93.2 %collective-permute-start.5 = (bf16[512,2560]{1,0:T(8,128)(2,1)}, bf16[512,2560]{1,0:T(8,128)(2,1)}, u32[]{:S(2)}, u32[]{:S(2)}) collective-permute-start(bf16[512,2560]{1,0:T(8,128)(2,1)} %collective-permute-done.4.refs_0_), channel_id=1, source_target_pairs={{0,1},{1,0},{2,3},{3,2},{4,5},{5,4},{6,7},{7,6}} | collective-permute-start | bytes 7864328 | tf_op jit(solution)/shard_map/ppermute | solution.py:446
